TPU v7x, 32 devices: a whole 2x2x4 slice. The times are simulated.
32 devices in a mesh: groups: 2 (over y), seq: 4 (over x, core), tensor: 4 (over z).
Axes of the slice: x: 2, y: 2, z: 4, core: 2. Of those that a mesh axis runs over, the one named last changes fastest.
Arguments:
- hidden: bfloat16 [256, 4608], P(('groups', 'seq')), parts along dimension 0, may hold values from -6 to 6
- pre_gain: float32 [4608], replicated, may hold values from 0.25 to 1.75
- w_query: bfloat16 [4608, 4096], P(None, 'tensor'), may hold values from -0.09375 to 0.09375
- w_key: bfloat16 [4608, 2048], P(None, 'tensor'), may hold values from -0.09375 to 0.09375
- w_value: bfloat16 [4608, 2048], P(None, 'tensor'), may hold values from -0.09375 to 0.09375
- w_out: bfloat16 [4096, 4608], P('tensor'), may hold values from -0.125 to 0.125
- post_gain: float32 [4608], P('tensor'), may hold values from 0.25 to 1.75
- cache_pool: bfloat16 [512, 2, 128, 2048], P(('groups', 'seq'), None, None, 'tensor'), parts along dimension 0, may hold values from -6 to 6
- prompt_cache: bfloat16 [256, 2, 64, 2048], P('seq', None, None, 'tensor'), may hold values from -6 to 6
- task_ids: int32 [256], P('groups'), parts along dimension 0, may hold values from 0 to 255
- cache_lengths: int32 [256], P('groups'), parts along dimension 0, may hold values from 1 to 4096, as said below
- block_table: int32 [256, 32], P('groups'), parts along dimension 0, may hold values from -1 to 255, as said below
Outputs:
- layer_out: bfloat16 [256, 4608], P(('groups', 'seq'), 'tensor'), parts along dimension 0
- fresh_cache: bfloat16 [256, 2, 2048], P(('groups', 'seq'), None, 'tensor'), parts along dimension 0
There are 2 independent parts, one for each index of `groups`. A program takes and returns all parts, laid end to end along the dimension named above; an argument that names none is the same for every part. Nothing has to cross between parts.
Inputs may be any that keep to these rules, and one draw needn't show every extreme that they name: `cache_lengths`: each draw has a request with exactly 4096 cache tokens. block_table[r, j] is the page of cache_pool holding cache tokens j * 128 to (j + 1) * 128 - 1 of request r for j < ceil(cache_lengths[r] / 128), and -1 for the later j; no page is named twice.
All inputs are finite; a program needn't handle non-finite values.
Results may differ from a plain program's by a relative error of at most 0.018.
Values may be sent and summed in bfloat16 or wider, within the bound.
No kernel may reach another device: no remote copies, remote signals or barrier semaphores. Data moves between devices by JAX's collectives and lax.ppermute only.
A program may use at most 128 MiB of HBM per device.

v0:
```python
import jax
import jax.numpy as jnp
from jax import lax
from jax.sharding import PartitionSpec as P

D = 4608
H = 32
HD = 128


cap_limit = 50.0


def rms_scale(values, gain):
    mean_square = jnp.mean(values * values, axis=-1, keepdims=True)
    return values * lax.rsqrt(mean_square + 1e-06) * gain


def rotate(values, position):
    half_dim = values.shape[-1] // 2
    frequency = 10000.0 ** (-jnp.arange(half_dim, dtype=jnp.float32) / half_dim)
    angles = position.astype(jnp.float32)[:, None] * frequency[None, :]
    cosine = jnp.cos(angles)[:, None, :]
    sines = jnp.sin(angles)[:, None, :]
    first_half = values[..., :half_dim]
    second_half = values[..., half_dim:]
    return jnp.concatenate(
        [first_half * cosine - second_half * sines, second_half * cosine + first_half * sines],
        axis=-1,
    )


def capped(raw_score, score_scale):
    return cap_limit * jnp.tanh(raw_score * score_scale / cap_limit)


def attend(query_block, block, live_mask, score_scale):
    count = block.shape[0]
    length = block.shape[2]
    kv_heads = query_block.shape[1]
    head_dim = query_block.shape[3]
    block_keys = block[:, 0].reshape(count, length, kv_heads, head_dim)
    block_values = block[:, 1].reshape(count, length, kv_heads, head_dim)
    raw_score = jnp.einsum(
        "nkgd,ntkd->nkgt", query_block, block_keys, preferred_element_type=jnp.float32
    )
    weight = jnp.where(live_mask[:, None, None, :], jnp.exp(capped(raw_score, score_scale)), 0.0)
    totals = jnp.sum(weight, axis=-1).reshape(count, -1)
    mixtures = jnp.einsum(
        "nkgt,ntkd->nkgd",
        weight.astype(jnp.bfloat16),
        block_values,
        preferred_element_type=jnp.float32,
    )
    return (totals, mixtures.reshape(count, -1))


def body(
    hidden,
    pre_gain,
    w_query,
    w_key,
    w_value,
    w_out,
    post_gain,
    cache_pool,
    prompt_cache,
    task_ids,
    cache_lengths,
    block_table,
):
    seq_index = lax.axis_index("seq")
    tensor_index = lax.axis_index("tensor")
    own_rows = hidden.shape[0]
    requests = task_ids.shape[0]
    pages_dev = cache_pool.shape[0]
    block_len = cache_pool.shape[2]
    kv_width = cache_pool.shape[3]
    head_dim = HD
    kv_heads = kv_width // head_dim
    query_heads = w_query.shape[1] // head_dim
    group_size = query_heads // kv_heads
    prompt_len = prompt_cache.shape[2]
    tasks_dev = prompt_cache.shape[0]
    score_scale = float(D // H) ** (-0.5)
    first_row = seq_index * own_rows
    own_lengths = lax.dynamic_slice_in_dim(cache_lengths, first_row, own_rows)
    normed = rms_scale(hidden.astype(jnp.float32), pre_gain).astype(jnp.bfloat16)
    position = prompt_len + own_lengths
    query_rows = rotate(
        jnp.dot(normed, w_query, preferred_element_type=jnp.float32).reshape(
            own_rows, query_heads, head_dim
        ),
        position,
    ).astype(jnp.bfloat16)
    key_new = rotate(
        jnp.dot(normed, w_key, preferred_element_type=jnp.float32).reshape(
            own_rows, kv_heads, head_dim
        ),
        position,
    ).astype(jnp.bfloat16)
    value_new = jnp.dot(normed, w_value, preferred_element_type=jnp.float32).astype(jnp.bfloat16)
    fresh_cache = jnp.stack([key_new.reshape(own_rows, kv_width), value_new], axis=1)
    queries = lax.all_gather(
        query_rows.reshape(own_rows, query_heads * head_dim), "seq", axis=0, tiled=True
    )
    page_ids = seq_index * pages_dev + jnp.arange(pages_dev)
    flat_table = block_table.reshape(-1)
    max_blocks = block_table.shape[1]
    matches = flat_table[None, :] == page_ids[:, None]
    entry_index = jnp.arange(flat_table.shape[0])
    page_used = jnp.any(matches, axis=1)
    found_entry = jnp.sum(jnp.where(matches, entry_index[None, :], 0), axis=1)
    page_owner = found_entry // max_blocks
    block_number = found_entry % max_blocks
    owner_hot = (page_owner[:, None] == jnp.arange(requests)[None, :]) & page_used[:, None]
    owner_length = jnp.sum(jnp.where(owner_hot, cache_lengths[None, :], 0), axis=1)
    valid_count = jnp.clip(owner_length - block_number * block_len, 0, block_len)
    page_query = jnp.dot(
        owner_hot.astype(jnp.bfloat16), queries, preferred_element_type=jnp.float32
    ).astype(jnp.bfloat16)
    page_query = page_query.reshape(pages_dev, kv_heads, group_size, head_dim)
    page_live = jnp.arange(block_len)[None, :] < valid_count[:, None]
    page_totals, page_mixtures = attend(page_query, cache_pool, page_live, score_scale)
    spread_hot = owner_hot.astype(jnp.float32).T
    totals = jnp.dot(spread_hot, page_totals, precision=lax.Precision.HIGHEST)
    mixtures = jnp.dot(spread_hot, page_mixtures, precision=lax.Precision.HIGHEST)
    local_task = task_ids - seq_index * tasks_dev
    is_owned = (local_task >= 0) & (local_task < tasks_dev)
    task_rows = prompt_cache[jnp.clip(local_task, 0, tasks_dev - 1)]
    all_query = queries.reshape(requests, kv_heads, group_size, head_dim)
    owned_live = jnp.broadcast_to(is_owned[:, None], (requests, prompt_len))
    prompt_totals, prompt_mixtures = attend(all_query, task_rows, owned_live, score_scale)
    totals = totals + prompt_totals
    mixtures = mixtures + prompt_mixtures
    totals, mixtures = (
        lax.psum_scatter(
            totals.astype(jnp.bfloat16), "seq", scatter_dimension=0, tiled=True
        ).astype(jnp.float32),
        lax.psum_scatter(
            mixtures.astype(jnp.bfloat16), "seq", scatter_dimension=0, tiled=True
        ).astype(jnp.float32),
    )
    own_query = query_rows.reshape(own_rows, kv_heads, group_size, head_dim)
    self_raw = jnp.sum(
        own_query.astype(jnp.float32) * key_new[:, :, None, :].astype(jnp.float32), axis=-1
    )
    self_weight = jnp.exp(capped(self_raw, score_scale))
    rounded = lax.optimization_barrier(self_weight.astype(jnp.bfloat16)).astype(jnp.float32)
    totals = totals + self_weight.reshape(own_rows, -1)
    self_mix = rounded[..., None] * value_new.reshape(own_rows, kv_heads, 1, head_dim).astype(
        jnp.float32
    )
    mixtures = mixtures + self_mix.reshape(own_rows, -1)
    attended = (mixtures.reshape(own_rows, query_heads, head_dim) / totals[..., None]).astype(
        jnp.bfloat16
    )
    projected = jnp.dot(
        attended.reshape(own_rows, query_heads * head_dim),
        w_out,
        preferred_element_type=jnp.float32,
    )
    cols_local = post_gain.shape[0]
    col_start = tensor_index * cols_local
    residual = lax.dynamic_slice_in_dim(hidden, col_start, cols_local, 1).astype(jnp.float32)
    whole_sum = lax.psum(projected.astype(jnp.bfloat16), "tensor").astype(jnp.float32)
    mean_square = jnp.mean(whole_sum * whole_sum, axis=1, keepdims=True)
    scaled = lax.dynamic_slice_in_dim(whole_sum, col_start, cols_local, 1) * lax.rsqrt(
        mean_square + 1e-06
    )
    layer_out = (residual + scaled * post_gain).astype(jnp.bfloat16)
    return (layer_out, fresh_cache)


def solution(mesh):
    return jax.shard_map(
        body,
        mesh=mesh,
        in_specs=(
            P(("groups", "seq"), None),
            P(),
            P(None, "tensor"),
            P(None, "tensor"),
            P(None, "tensor"),
            P("tensor", None),
            P("tensor"),
            P(("groups", "seq"), None, None, "tensor"),
            P("seq", None, None, "tensor"),
            P("groups"),
            P("groups"),
            P("groups", None),
        ),
        out_specs=(P(("groups", "seq"), "tensor"), P(("groups", "seq"), None, "tensor")),
        check_vma=False,
    )
```

profile of v0, /device:TPU:0, one launch (start us, length us, event | category | flops | bytes accessed | tf_op | source)
XLA Modules:
  0.0 237.7 jit_solution(1998318495962879514)
XLA Ops:
  7.2 0.7 compare_select_fusion.1
  7.9 0.7 compare_and_fusion
  8.6 0.8 copy.81
  10.1 1.1 fusion.11
  11.2 5.6 %convolution_bitcast_fusion = f32[4,8,8,128]{3,1,2,0:T(8,128)S(1)} fusion(bf16[4608,1024]{1,0:T(8,128)(2,1)} %param.14, bf16[32,4608]{1,0:T(8,128)(2,1)} %param.12, f32[4608]{0:T(1024)} %param.13, f32[32]{0:T(128)S(1)} %add_rsqrt_fusion.1), kind=kOutput, calls=%fused_computation.17 | convolution fusion | flops 302579712 | bytes 9881728 | tf_op jit(solution)/shard_map/dot_general | solution.py:91
  17.3 7.2 %all_gather.3 = bf16[128,1024]{1,0:T(8,128)(2,1)S(1)} all-gather(bf16[32,1024]{1,0:T(8,128)(2,1)S(1)} %bitcast.48), channel_id=1, replica_groups=mesh['groups'=2,'seq'=4,'tensor'=4] {'seq'}, dimensions={0}, use_global_device_ids=true | all-gather | bytes 327680 | tf_op jit(solution)/shard_map/all_gather | solution.py:104
  25.2 11.3 %gather_fusion = bf16[128,2,64,512]{3,2,1,0:T(8,128)(2,1)} fusion(bf16[64,2,64,512]{3,2,1,0:T(8,128)(2,1)} %param.20, s32[1024]{0:T(1024)S(1)} %pad_clamp_fusion), kind=kCustom, calls=%fused_computation | custom fusion | bytes 33554944 | tf_op jit(solution)/shard_map/gather | solution.py:130
  36.5 11.7 %fusion.40 = (bf16[128,1,64,512]{3,2,1,0:T(8,128)(2,1)}, bf16[128,1,64,512]{3,2,1,0:T(8,128)(2,1)}) fusion(bf16[128,2,64,512]{3,2,1,0:T(8,128)(2,1)} %gather_fusion), kind=kLoop, calls=%fused_computation.79 | loop fusion | bytes 33554432 | tf_op jit(solution)/shard_map/slice | solution.py:43
  48.2 13.0 %copy.86 = bf16[128,1,64,512]{0,3,2,1:T(8,128)(2,1)} copy(bf16[128,1,64,512]{3,2,1,0:T(8,128)(2,1)} %get-tuple-element.21) | data formatting | bytes 16777216 | tf_op jit(solution)/shard_map/slice | solution.py:42
  61.1 12.0 %copy.87 = bf16[128,64,4,128]{3,1,2,0:T(8,128)(2,1)} copy(bf16[128,64,4,128]{0,3,2,1:T(8,128)(2,1)} %bitcast.41) | data formatting | bytes 16777216 | tf_op jit(solution)/shard_map/reshape;squeeze | solution.py:42
  73.1 8.0 %fusion.41 = (f32[128,4,2]{2,1,0:T(4,128)S(1)}, bf16[128,4,2,64]{3,2,1,0:T(2,128)(2,1)S(1)}) fusion(bf16[128,4,2,128]{3,2,1,0:T(2,128)(2,1)S(1)} %reshape.222, bf16[128,64,4,128]{3,1,2,0:T(8,128)(2,1)} %copy.87, pred[128]{0:T(512)(128)(4,1)S(1)} %compare_and_fusion), kind=kOutput, calls=%fused_computation.80 | convolution fusion | flops 17103872 | bytes 8786048 | tf_op jit(solution)/shard_map/nkgd,ntkd->nkgt/dot_general | solution.py:44
  81.3 11.6 %fusion.39 = (bf16[64,1,128,512]{3,2,1,0:T(8,128)(2,1)}, bf16[64,1,128,512]{3,2,1,0:T(8,128)(2,1)}) fusion(bf16[64,2,128,512]{3,2,1,0:T(8,128)(2,1)} %param.19), kind=kLoop, calls=%fused_computation.78 | loop fusion | bytes 33554432 | tf_op jit(solution)/shard_map/slice | solution.py:43
  92.9 11.9 %copy.101 = bf16[64,1,128,512]{2,3,0,1:T(8,128)(2,1)} copy(bf16[64,1,128,512]{3,2,1,0:T(8,128)(2,1)} %get-tuple-element.19) | data formatting | bytes 16777216
  104.9 5.8 %fusion.42 = (f32[64,4,2]{2,1,0:T(4,128)S(1)}, bf16[64,4,2,128]{3,2,1,0:T(2,128)(2,1)S(1)}) fusion(bf16[64,4,2,128]{3,2,1,0:T(2,128)(2,1)S(1)} %reshape.220, bf16[64,128,4,128]{1,3,2,0:T(8,128)(2,1)} %bitcast.39, pred[64,128]{1,0:T(8,128)(4,1)S(1)} %iota_compare_fusion), kind=kOutput, calls=%fused_computation.81 | convolution fusion | flops 17104384 | bytes 8660992 | tf_op jit(solution)/shard_map/nkgd,ntkd->nkgt/dot_general | solution.py:44
  111.0 0.7 copy.99
  112.0 13.0 %copy.88 = bf16[128,1,64,512]{0,3,2,1:T(8,128)(2,1)} copy(bf16[128,1,64,512]{3,2,1,0:T(8,128)(2,1)} %get-tuple-element.20) | data formatting | bytes 16777216 | tf_op jit(solution)/shard_map/slice | solution.py:43
  125.0 12.0 %copy.89 = bf16[128,64,4,128]{3,1,2,0:T(8,128)(2,1)} copy(bf16[128,64,4,128]{0,3,2,1:T(8,128)(2,1)} %bitcast.42) | data formatting | bytes 16777216 | tf_op jit(solution)/shard_map/reshape;squeeze | solution.py:43
  137.1 5.6 %fusion.14 = f32[128,4,2,128]{3,2,1,0:T(2,128)S(1)} fusion(bf16[128,64,4,128]{3,1,2,0:T(8,128)(2,1)} %copy.89, bf16[128,4,2,64]{3,2,1,0:T(2,128)(2,1)S(1)} %get-tuple-element.31), kind=kOutput, calls=%fused_computation.28 | convolution fusion | flops 16777216 | bytes 9043968 | tf_op jit(solution)/shard_map/nkgt,ntkd->nkgd/dot_general | solution.py:49
  142.7 0.4 reshape.223
  143.1 11.9 %copy.102 = bf16[64,1,128,512]{2,3,0,1:T(8,128)(2,1)} copy(bf16[64,1,128,512]{3,2,1,0:T(8,128)(2,1)} %get-tuple-element.18) | data formatting | bytes 16777216
  155.0 7.8 %fusion.17 = f32[64,4,2,128]{3,2,1,0:T(2,128)S(1)} fusion(bf16[64,128,4,128]{1,3,2,0:T(8,128)(2,1)} %bitcast.40, bf16[64,4,2,128]{3,2,1,0:T(2,128)(2,1)S(1)} %get-tuple-element.33), kind=kOutput, calls=%fused_computation.34 | convolution fusion | flops 16777216 | bytes 8781824 | tf_op jit(solution)/shard_map/nkgt,ntkd->nkgd/dot_general | solution.py:49
  163.1 1.2 fusion.4
  164.4 3.3 %fusion.35 = f32[32,512]{1,0:T(8,128)S(1)} fusion(bf16[4608,512]{1,0:T(8,128)(2,1)} %param.15, bf16[32,4608]{1,0:T(8,128)(2,1)S(1)} %copy-done, f32[4608]{0:T(1024)S(1)} %copy-done.1, f32[32]{0:T(128)S(1)} %add_rsqrt_fusion.1), kind=kOutput, calls=%fused_computation.76 | convolution fusion | flops 151584768 | bytes 5097600 | tf_op jit(solution)/shard_map/dot_general | solution.py:97
  168.4 3.3 %convolution_convert_fusion.2 = bf16[32,512]{1,0:T(8,128)(2,1)S(1)} fusion(bf16[4608,512]{1,0:T(8,128)(2,1)} %param.16, bf16[32,4608]{1,0:T(8,128)(2,1)S(1)} %copy-done, f32[4608]{0:T(1024)S(1)} %copy-done.1, f32[32]{0:T(128)S(1)} %add_rsqrt_fusion.1), kind=kOutput, calls=%fused_computation.18 | convolution fusion | flops 151601152 | bytes 5064832 | tf_op jit(solution)/shard_map/dot_general | solution.py:102
  172.3 0.8 copy.100
  173.1 12.8 %reduce-scatter.5.cloned.1.call-done = bf16[32,1024]{1,0:T(8,128)(2,1)} async-done(((bf16[128,1024]{1,0:T(8,128)(2,1)}), bf16[32,1024]{1,0:T(8,128)(2,1)}) %reduce-scatter.5.cloned.1.call-update) | async-done | bytes 65552 | tf_op jit(solution)/shard_map/reduce_scatter | solution.py:140
  186.0 6.1 %convolution_convert_fusion = bf16[32,4608]{1,0:T(8,128)(2,1)} fusion(bf16[1024,4608]{1,0:T(8,128)(2,1)} %param.17, f32[4,8,8,128]{3,2,1,0:T(8,128)S(1)} %bitcast.44, f32[32,1024]{1,0:T(8,128)S(1)} %mul.214, bf16[32,1024]{1,0:T(8,128)(2,1)} %reduce-scatter.5.cloned.1.call-done), kind=kOutput, calls=%fused_computation.1 | convolution fusion | flops 302268416 | bytes 10059776 | tf_op jit(solution)/shard_map/dot_general | solution.py:158
  192.2 0.7 copy.96
  192.9 35.4 %all-reduce.2.cloned.1.call-done = bf16[32,4608]{1,0:T(8,128)(2,1)} async-done(((bf16[32,4608]{1,0:T(8,128)(2,1)}), bf16[32,4608]{1,0:T(8,128)(2,1)}) %all-reduce.2.cloned.1.call-update) | async-done | bytes 294928 | tf_op jit(solution)/shard_map/psum | solution.py:166
  228.3 1.1 multiply_reduce_fusion
  229.5 1.0 convert_element_type.125
  230.5 0.7 add_convert_fusion
  (56 shorter events, 4.4 us)
Async XLA Ops:
  7.2 165.1 %reduce-scatter.7.cloned.1.call-start = ((), (), s32[]{:S(2)}) async-start(), calls=%async_computation.4 | async-start | bytes 40960
  11.2 5.7 %copy-start.3 = (s32[128]{0:T(128)S(1)}, s32[128]{0:T(128)}, u32[]{:S(2)}) copy-start(s32[128]{0:T(128)} %param.22) | copy-start | bytes 1540
  111.8 74.1 %reduce-scatter.5.cloned.1.call-start = ((), (), s32[]{:S(2)}) async-start(), calls=%async_computation.2 | async-start | bytes 327680 | tf_op jit(solution)/shard_map/reduce_scatter | solution.py:140
  155.0 9.3 %copy-start = (bf16[32,4608]{1,0:T(8,128)(2,1)S(1)}, bf16[32,4608]{1,0:T(8,128)(2,1)}, u32[]{:S(2)}) copy-start(bf16[32,4608]{1,0:T(8,128)(2,1)} %param.12) | copy-start | bytes 884740
  155.0 9.3 %copy-start.1 = (f32[4608]{0:T(1024)S(1)}, f32[4608]{0:T(1024)}, u32[]{:S(2)}) copy-start(f32[4608]{0:T(1024)} %param.13) | copy-start | bytes 55300
  164.3 64.0 %all-reduce.2.cloned.1.call-start = ((), (), s32[]{:S(2)}) async-start(), calls=%async_computation.3 | async-start | bytes 589824 | tf_op jit(solution)/shard_map/psum | solution.py:166
  186.0 44.5 %copy-start.2 = (f32[1152]{0:T(1024)S(1)}, f32[1152]{0:T(1024)}, u32[]{:S(2)}) copy-start(f32[1152]{0:T(1024)} %param.18) | copy-start | bytes 13828
Sparse Core Ops, SparseCore 0:
  111.9 20.9 reduce-scatter.6
  164.4 21.4 reduce-scatter.4
  192.3 35.9 all-reduce.1
where the time goes:
time: 240 us; the launch traced here: 238 us
  local copies, waits for them, and re-layouts  113 us (47%)
  waiting for transfers between devices  48.3 us (20%)
  matrix products  47.2 us (20%)
  between operations  14 us (6%)
  other arithmetic  7.5 us (3%)
  blocking collectives  7.22 us (3%)
    slice x3, local copies, waits for them, and re-layouts, attend(): block_values = block[:, 1].reshape(count, length, kv_heads, head_dim)  36.3 us
    psum x1, waiting for transfers between devices, body(): lax.psum(projected.astype(jnp.bfloat16), 'tensor').astype(jnp.float32)  35.4 us
    unnamed x16, local copies, waits for them, and re-layouts  26.8 us
    dot_general x2, matrix products, attend(): jnp.einsum('nkgd,ntkd->nkgt', query_block, block_keys, preferred_element_...  13.8 us
    dot_general x2, matrix products, attend(): jnp.einsum('nkgt,ntkd->nkgd', weight.astype(jnp.bfloat16), block_values,...  13.5 us
    slice x1, local copies, waits for them, and re-layouts, attend(): block_keys = block[:, 0].reshape(count, length, kv_heads, head_dim)  13 us
    reduce_scatter x1, waiting for transfers between devices, body(): lax.psum_scatter(mixtures.astype(jnp.bfloat16), 'seq', scatter_dimension=...  12.8 us
    another operation x1, local copies, waits for them, and re-layouts, attend(): block_values = block[:, 1].reshape(count, length, kv_heads, head_dim)  12 us
  transfers between devices with their start and end apart: 3, of which 2 were waited for; matrix products, arithmetic and copies ran while one was open for 26% of the time, Pallas kernels for 0%

commit v1 on v0

--- a/solution.py
+++ b/solution.py
@@ -1,14 +1,21 @@
+import functools
+
 import jax
 import jax.numpy as jnp
 from jax import lax
+from jax.experimental import pallas as pl
+from jax.experimental.pallas import tpu as pltpu
 from jax.sharding import PartitionSpec as P
 
 D = 4608
 H = 32
 HD = 128
-
+LANES = 128
+SUB = 8
 
 cap_limit = 50.0
+F32 = jnp.float32
+BF16 = jnp.bfloat16
 
 
 def rms_scale(values, gain):
@@ -55,7 +62,7 @@
     return (totals, mixtures.reshape(count, -1))
 
 
-def body(
+def plain_body(
     hidden,
     pre_gain,
     w_query,
@@ -172,9 +179,491 @@
     return (layer_out, fresh_cache)
 
 
+VM = pl.BlockSpec(memory_space=pltpu.VMEM)
+SM = pl.BlockSpec(memory_space=pltpu.SMEM)
+HB = pl.BlockSpec(memory_space=pltpu.HBM)
+
+
+def cost(flops):
+    return pl.CostEstimate(flops=flops, bytes_accessed=1 << 20, transcendentals=0)
+
+
+def row_iota(rows):
+    return lax.broadcasted_iota(jnp.int32, (rows, LANES), 0)
+
+
+def lane_iota(rows):
+    return lax.broadcasted_iota(jnp.int32, (rows, LANES), 1)
+
+
+def query_kernel(prompt_len, chunks, lens_ref, hidden_ref, gain_ref, w_ref, q_ref, n_ref, cs_ref, w_buf, sem):
+    rows, depth = hidden_ref.shape
+    width = q_ref.shape[1]
+    step = depth // chunks
+    copies = []
+    for c in range(chunks):
+        part = pl.ds(c * step, step)
+        copy = pltpu.make_async_copy(w_ref.at[part, :], w_buf.at[part, :], sem.at[c])
+        copy.start()
+        copies.append(copy)
+    x = hidden_ref[...].astype(F32)
+    mean_square = jnp.sum(x * x, axis=-1, keepdims=True) / depth
+    n_ref[...] = (x * lax.rsqrt(mean_square + 1e-06) * gain_ref[...]).astype(BF16)
+    first = lax.axis_index("seq") * rows
+    row = row_iota(rows)
+    lane = lane_iota(rows)
+    length = jnp.zeros((rows, LANES), jnp.int32)
+    for i in range(rows):
+        length = jnp.where(row == i, lens_ref[first + i], length)
+    half = LANES // 2
+    low = lane < half
+    slot = jnp.where(low, lane, lane - half).astype(F32)
+    frequency = jnp.exp(slot * (-9.210340371976184 / half))
+    angles = (length + prompt_len).astype(F32) * frequency
+    cosine = jnp.cos(angles)
+    sines = jnp.where(low, -jnp.sin(angles), jnp.sin(angles))
+    cs_ref[:, :LANES] = cosine
+    cs_ref[:, LANES:] = sines
+    total = jnp.zeros((rows, width), F32)
+    for c in range(chunks):
+        copies[c].wait()
+        total = total + jnp.dot(
+            n_ref[:, c * step : (c + 1) * step],
+            w_buf[c * step : (c + 1) * step, :],
+            preferred_element_type=F32,
+        )
+    for h in range(width // LANES):
+        v = total[:, h * LANES : (h + 1) * LANES]
+        q_ref[:, h * LANES : (h + 1) * LANES] = (
+            v * cosine + pltpu.roll(v, half, 1) * sines
+        ).astype(BF16)
+
+
+def plan_kernel(pages, block_len, tasks, table_ref, lens_ref, task_ref, meta_ref):
+    requests = lens_ref.shape[0]
+    seq = lax.axis_index("seq")
+    page0 = seq * pages
+    task0 = seq * tasks
+
+    def clear(i, c):
+        meta_ref[i] = 0
+        return c
+
+    lax.fori_loop(0, meta_ref.shape[0], clear, 0, unroll=8)
+
+    def request(r, count):
+        length = lens_ref[r]
+        blocks = (length + block_len - 1) // block_len
+
+        def block(j, c):
+            page = table_ref[j, r] - page0
+
+            @pl.when((page >= 0) & (page < pages))
+            def _():
+                meta_ref[page] = r
+                meta_ref[pages + page] = jnp.minimum(length - j * block_len, block_len)
+
+            return c
+
+        lax.fori_loop(0, blocks, block, 0)
+        task = task_ref[r] - task0
+        here = (task >= 0) & (task < tasks)
+
+        @pl.when(here)
+        def _():
+            meta_ref[2 * pages + count] = r
+            meta_ref[2 * pages + requests + count] = task
+
+        return count + here.astype(jnp.int32)
+
+    count = lax.fori_loop(0, requests, request, 0)
+    meta_ref[2 * pages + 2 * requests] = count
+
+
+def attend_kernel(
+    n_seq, score_scale, batch,
+    meta_hbm, q_refs, pages_ref, prompt_ref, own_ref, msg_refs, meta_ref, qf, acc, acw, sem,
+):
+    rows, width = q_refs[0].shape
+    heads = width // LANES
+    pages, _, block_len, kv_width = pages_ref.shape
+    kvh = kv_width // LANES
+    group = heads // kvh
+    prompt_len = prompt_ref.shape[2]
+    requests = rows * n_seq
+    me = lax.axis_index("seq")
+    fetch = pltpu.make_async_copy(meta_hbm, meta_ref, sem)
+    fetch.start()
+    acc[...] = jnp.zeros_like(acc)
+    acw[...] = jnp.zeros_like(acw)
+    for k in range(n_seq):
+        base = pl.multiple_of((me ^ k) * (rows * heads), SUB)
+        for h in range(heads):
+            qf[pl.ds(base + h, rows, stride=heads), :] = q_refs[k][
+                :, h * LANES : (h + 1) * LANES
+            ].astype(F32)
+    fetch.wait()
+    sub = row_iota(heads) // group
+    lane = lane_iota(heads)
+    zero = jnp.zeros((heads, LANES), F32)
+
+    def spread(r):
+        q = qf[pl.ds(pl.multiple_of(r * heads, SUB), heads), :]
+        return jnp.concatenate([jnp.where(sub == g, q, zero) for g in range(kvh)], axis=1)
+
+    def weigh(s, live):
+        w = jnp.exp(cap_limit * jnp.tanh(s * (score_scale / cap_limit)))
+        return jnp.where(live, w, zero)
+
+    def collect(o):
+        out = zero
+        for g in range(kvh):
+            out = jnp.where(sub == g, o[:, g * LANES : (g + 1) * LANES], out)
+        return out
+
+    def add(r, w, o):
+        at = pl.ds(pl.multiple_of(r * heads, SUB), heads)
+        acw[at, :] = acw[at, :] + w
+        acc[at, :] = acc[at, :] + o
+
+    pair = 2
+
+    def page_step(i, c):
+        owners, weights, values = [], [], []
+        for b in range(batch):
+            p = (i * batch + b) * pair
+            who = [meta_ref[p + j] for j in range(pair)]
+            q2 = jnp.concatenate([spread(r) for r in who], axis=0).astype(BF16)
+            keys = pages_ref[pl.ds(p, pair), 0].reshape(pair * block_len, kv_width)
+            s = lax.dot_general(q2, keys, (((1,), (1,)), ((), ())), preferred_element_type=F32)
+            ws = []
+            for j in range(pair):
+                live = lane < meta_ref[pages + p + j]
+                ws.append(weigh(s[j * heads : (j + 1) * heads, j * block_len : (j + 1) * block_len], live))
+            owners.append(who)
+            weights.append(ws)
+        for b in range(batch):
+            p = (i * batch + b) * pair
+            ws = weights[b]
+            w2 = jnp.concatenate(
+                [
+                    jnp.concatenate([ws[j] if m == j else zero for m in range(pair)], axis=1)
+                    for j in range(pair)
+                ],
+                axis=0,
+            ).astype(BF16)
+            vals = pages_ref[pl.ds(p, pair), 1].reshape(pair * block_len, kv_width)
+            values.append(jnp.dot(w2, vals, preferred_element_type=F32))
+        for b in range(batch):
+            for j in range(pair):
+                add(owners[b][j], weights[b][j], collect(values[b][j * heads : (j + 1) * heads]))
+        return c
+
+    lax.fori_loop(0, pages // (pair * batch), page_step, 0)
+
+    count = meta_ref[2 * pages + 2 * requests]
+    per = LANES // prompt_len
+    quad = 2 * per
+    pbatch = 2
+
+    def prompt_step(i, c):
+        owners, weights, values, tasks = [], [], [], []
+        for b in range(pbatch):
+            e = (i * pbatch + b) * quad
+            who = [meta_ref[2 * pages + e + j] for j in range(quad)]
+            task = [meta_ref[2 * pages + requests + e + j] for j in range(quad)]
+            q4 = jnp.concatenate([spread(r) for r in who], axis=0).astype(BF16)
+            keys = jnp.concatenate([prompt_ref[t, 0] for t in task], axis=0)
+            s = lax.dot_general(q4, keys, (((1,), (1,)), ((), ())), preferred_element_type=F32)
+            ws = []
+            for j in range(quad):
+                tile = j // per
+                live = (lane // prompt_len == j % per) & (e + j < count)
+                ws.append(weigh(s[j * heads : (j + 1) * heads, tile * LANES : (tile + 1) * LANES], live))
+            owners.append(who)
+            weights.append(ws)
+            tasks.append(task)
+        for b in range(pbatch):
+            ws = weights[b]
+            w4 = jnp.concatenate(
+                [
+                    jnp.concatenate([ws[j] if m == j // per else zero for m in range(2)], axis=1)
+                    for j in range(quad)
+                ],
+                axis=0,
+            ).astype(BF16)
+            vals = jnp.concatenate([prompt_ref[t, 1] for t in tasks[b]], axis=0)
+            values.append(jnp.dot(w4, vals, preferred_element_type=F32))
+        for b in range(pbatch):
+            for j in range(quad):
+                add(owners[b][j], weights[b][j], collect(values[b][j * heads : (j + 1) * heads]))
+        return c
+
+    lax.fori_loop(0, (count + quad * pbatch - 1) // (quad * pbatch), prompt_step, 0)
+
+    lanes = lane_iota(rows)
+    for k in range(n_seq):
+        base = (me ^ k) * (rows * heads)
+        sums = jnp.zeros((rows, LANES), F32)
+        for h in range(heads):
+            at = pl.ds(base + h, rows, stride=heads)
+            mix = acc[at, :]
+            tot = jnp.sum(acw[at, :], axis=1, keepdims=True)
+            if k == 0:
+                own_ref[:, h * LANES : (h + 1) * LANES] = mix
+                sums = jnp.where(lanes == h, tot, sums)
+            else:
+                msg_refs[k - 1][:, h * LANES : (h + 1) * LANES] = mix.astype(BF16)
+                top = tot.astype(BF16).astype(F32)
+                sums = jnp.where(lanes == h, top, jnp.where(lanes == heads + h, tot - top, sums))
+        if k == 0:
+            own_ref[:, heads * LANES :] = sums
+        else:
+            msg_refs[k - 1][:, heads * LANES :] = sums.astype(BF16)
+
+
+def fresh_kernel(score_scale, n_ref, cs_ref, q_ref, wk_ref, wv_ref, k_ref, v_ref, self_ref):
+    rows, width = q_ref.shape
+    heads = width // LANES
+    kvh = k_ref.shape[1] // LANES
+    group = heads // kvh
+    half = LANES // 2
+    normed = n_ref[...]
+    cosine = cs_ref[:, :LANES]
+    sines = cs_ref[:, LANES:]
+    keys = jnp.dot(normed, wk_ref[...], preferred_element_type=F32)
+    values = jnp.dot(normed, wv_ref[...], preferred_element_type=F32)
+    lanes = lane_iota(rows)
+    sums = jnp.zeros((rows, LANES), F32)
+    for g in range(kvh):
+        at = slice(g * LANES, (g + 1) * LANES)
+        key = keys[:, at]
+        key = (key * cosine + pltpu.roll(key, half, 1) * sines).astype(BF16)
+        k_ref[:, at] = key
+        key = key.astype(F32)
+        val = values[:, at].astype(BF16)
+        v_ref[:, at] = val
+        val = val.astype(F32)
+        for j in range(group):
+            h = g * group + j
+            raw = jnp.sum(q_ref[:, h * LANES : (h + 1) * LANES].astype(F32) * key, axis=1, keepdims=True)
+            w = jnp.exp(cap_limit * jnp.tanh(raw * (score_scale / cap_limit)))
+            self_ref[:, h * LANES : (h + 1) * LANES] = w.astype(BF16).astype(F32) * val
+            sums = jnp.where(lanes == h, w, sums)
+    self_ref[:, heads * LANES :] = sums
+
+
+def project_kernel(n_ten, w_ref, own_ref, self_ref, got_refs, p0_ref, out_refs):
+    rows, wide = own_ref.shape
+    heads = wide // LANES - 1
+    cols = p0_ref.shape[1]
+    at = slice(heads * LANES, (heads + 1) * LANES)
+    sums = own_ref[:, at] + self_ref[:, at]
+    tail = None
+    for r in got_refs:
+        got = r[:, at].astype(F32)
+        tail = got if tail is None else tail + got
+    parts = []
+    for h in range(heads):
+        at = slice(h * LANES, (h + 1) * LANES)
+        mix = own_ref[:, at] + self_ref[:, at]
+        for r in got_refs:
+            mix = mix + r[:, at].astype(F32)
+        tot = sums[:, h : h + 1]
+        if tail is not None:
+            tot = tot + tail[:, h : h + 1] + tail[:, heads + h : heads + h + 1]
+        parts.append((mix / tot).astype(BF16))
+    att = jnp.concatenate(parts, axis=1)
+    me = lax.axis_index("tensor")
+    for k in range(n_ten):
+        start = pl.multiple_of((me ^ k) * cols, LANES)
+        got = jnp.dot(att, w_ref[:, pl.ds(start, cols)], preferred_element_type=F32)
+        if k == 0:
+            p0_ref[...] = got
+        else:
+            out_refs[k - 1][...] = got.astype(BF16)
+
+
+def sum_kernel(p0_ref, got_refs, sum_ref, sq_ref):
+    rows, cols = p0_ref.shape
+    sq = jnp.zeros((rows, LANES), F32)
+    for c in range(cols // LANES):
+        at = slice(c * LANES, (c + 1) * LANES)
+        t = p0_ref[:, at]
+        for r in got_refs:
+            t = t + r[:, at].astype(F32)
+        sum_ref[:, at] = t
+        sq = sq + t * t
+    sq_ref[...] = sq
+
+
+def last_kernel(sum_ref, sq_ref, got_refs, hidden_ref, gain_ref, out_ref):
+    cols = out_ref.shape[1]
+    sq = sq_ref[...]
+    for r in got_refs:
+        sq = sq + r[...]
+    mean_square = jnp.sum(sq, axis=1, keepdims=True) / hidden_ref.shape[1]
+    start = pl.multiple_of(lax.axis_index("tensor") * cols, LANES)
+    residual = hidden_ref[:, pl.ds(start, cols)].astype(F32)
+    out_ref[...] = (
+        residual + sum_ref[...] * lax.rsqrt(mean_square + 1e-06) * gain_ref[...]
+    ).astype(BF16)
+
+
+def params(mib):
+    return pltpu.CompilerParams(vmem_limit_bytes=mib << 20)
+
+
+def swap(arrays, axis, size):
+    return [
+        lax.ppermute(a, axis, [(i, i ^ (k + 1)) for i in range(size)])
+        for k, a in enumerate(arrays)
+    ]
+
+
+def shape(dims, dtype):
+    return jax.ShapeDtypeStruct(dims, dtype)
+
+
+def fast_body(
+    n_seq,
+    n_ten,
+    hidden,
+    pre_gain,
+    w_query,
+    w_key,
+    w_value,
+    w_out,
+    post_gain,
+    cache_pool,
+    prompt_cache,
+    task_ids,
+    cache_lengths,
+    block_table,
+):
+    rows, depth = hidden.shape
+    width = w_query.shape[1]
+    kv_width = w_key.shape[1]
+    heads = width // LANES
+    pages, _, block_len, _ = cache_pool.shape
+    tasks, _, prompt_len, _ = prompt_cache.shape
+    requests = task_ids.shape[0]
+    cols = post_gain.shape[0]
+    wide = width + LANES
+    score_scale = float(D // H) ** (-0.5)
+    chunks = 9 if depth % 9 == 0 else 1
+    query, normed, cs = pl.pallas_call(
+        functools.partial(query_kernel, prompt_len, chunks),
+        out_shape=(shape((rows, width), BF16), shape((rows, depth), BF16), shape((rows, 2 * LANES), F32)),
+        in_specs=[SM, VM, VM, HB],
+        out_specs=(VM, VM, VM),
+        scratch_shapes=[pltpu.VMEM((depth, width), BF16), pltpu.SemaphoreType.DMA((chunks,))],
+        compiler_params=params(16),
+        cost_estimate=cost(1 << 28),
+        name="query",
+    )(cache_lengths, hidden, pre_gain.reshape(1, depth), pltpu.with_memory_space_constraint(w_query, pltpu.HBM))
+    got = swap([query] * (n_seq - 1), "seq", n_seq)
+    meta_len = 2 * pages + 2 * requests + LANES
+    meta = pl.pallas_call(
+        functools.partial(plan_kernel, pages, block_len, tasks),
+        out_shape=shape((meta_len,), jnp.int32),
+        in_specs=[SM, SM, SM],
+        out_specs=SM,
+        compiler_params=params(1),
+        cost_estimate=cost(1 << 28),
+        name="plan",
+    )(block_table.T, cache_lengths, task_ids)
+    batch = 4
+    outs = pl.pallas_call(
+        lambda meta_r, q0, q1, q2, q3, pg, pr, own, m1, m2, m3, *scratch: attend_kernel(
+            n_seq, score_scale, batch, meta_r, (q0, q1, q2, q3), pg, pr, own, (m1, m2, m3), *scratch
+        ),
+        out_shape=(shape((rows, wide), F32),) + (shape((rows, wide), BF16),) * (n_seq - 1),
+        in_specs=[HB] + [VM] * (n_seq + 2),
+        out_specs=(VM,) * n_seq,
+        scratch_shapes=[
+            pltpu.SMEM((meta_len,), jnp.int32),
+            pltpu.VMEM((requests * heads, LANES), F32),
+            pltpu.VMEM((requests * heads, LANES), F32),
+            pltpu.VMEM((requests * heads, LANES), F32),
+            pltpu.SemaphoreType.DMA,
+        ],
+        compiler_params=params(A_MIB),
+        cost_estimate=cost(1 << 30),
+        name="attend",
+    )(meta, query, *got, cache_pool, prompt_cache)
+    own, msgs = outs[0], outs[1:]
+    got = swap(msgs, "seq", n_seq)
+    key_new, value_new, self_part = pl.pallas_call(
+        functools.partial(fresh_kernel, score_scale),
+        out_shape=(shape((rows, kv_width), BF16), shape((rows, kv_width), BF16), shape((rows, wide), F32)),
+        in_specs=[VM] * 5,
+        out_specs=(VM,) * 3,
+        compiler_params=params(G_MIB),
+        cost_estimate=cost(1 << 29),
+        name="fresh",
+    )(normed, cs, query, w_key, w_value)
+    outs = pl.pallas_call(
+        lambda w, own, sf, r1, r2, r3, p0, o1, o2, o3: project_kernel(
+            n_ten, w, own, sf, (r1, r2, r3), p0, (o1, o2, o3)
+        ),
+        out_shape=(shape((rows, cols), F32),) + (shape((rows, cols), BF16),) * (n_ten - 1),
+        in_specs=[VM] * (3 + n_seq - 1),
+        out_specs=(VM,) * n_ten,
+        compiler_params=params(H_MIB),
+        cost_estimate=cost(1 << 29),
+        name="project",
+    )(w_out, own, self_part, *got)
+    p0, parts = outs[0], outs[1:]
+    got = swap(parts, "tensor", n_ten)
+    total, sq = pl.pallas_call(
+        lambda p0, r1, r2, r3, t, s: sum_kernel(p0, (r1, r2, r3), t, s),
+        out_shape=(shape((rows, cols), F32), shape((rows, LANES), F32)),
+        in_specs=[VM] * n_ten,
+        out_specs=(VM,) * 2,
+        compiler_params=params(2),
+        name="sum",
+    )(p0, *got)
+    got = swap([sq] * (n_ten - 1), "tensor", n_ten)
+    layer_out = pl.pallas_call(
+        lambda t, s, r1, r2, r3, hd, g, o: last_kernel(t, s, (r1, r2, r3), hd, g, o),
+        out_shape=shape((rows, cols), BF16),
+        in_specs=[VM] * (n_ten + 3),
+        out_specs=VM,
+        compiler_params=params(2),
+        name="last",
+    )(total, sq, *got, hidden, post_gain.reshape(1, cols))
+    fresh_cache = jnp.stack([key_new, value_new], axis=1)
+    return (layer_out, fresh_cache)
+
+
+A_MIB = 6
+G_MIB = 4
+H_MIB = 4
+
+
+def body(n_seq, n_ten, *args):
+    hidden, w_query, post_gain, cache_pool, prompt_cache = args[0], args[2], args[6], args[7], args[8]
+    fits = (
+        n_seq == 4
+        and n_ten == 4
+        and w_query.shape[1] == SUB * HD
+        and post_gain.shape[0] % LANES == 0
+        and cache_pool.shape[2] == LANES
+        and cache_pool.shape[0] % SUB == 0
+        and LANES % prompt_cache.shape[2] == 0
+        and prompt_cache.shape[2] % (2 * SUB) == 0
+        and args[9].shape[0] == hidden.shape[0] * n_seq
+        and hidden.shape[0] % (2 * SUB) == 0
+    )
+    if fits:
+        return fast_body(n_seq, n_ten, *args)
+    return plain_body(*args)
+
+
 def solution(mesh):
     return jax.shard_map(
-        body,
+        functools.partial(body, mesh.shape["seq"], mesh.shape["tensor"]),
         mesh=mesh,
         in_specs=(
             P(("groups", "seq"), None),

time: 240 us -> 59.2 us (0.25); the launches traced: 238 us -> 59.6 us
  local copies, waits for them, and re-layouts: 113 us -> 9.51 us
  matrix products: 47.2 us -> 0 us
  waiting for transfers between devices: 48.3 us -> 10.5 us
  Pallas kernels: 0 us -> 23 us
  starting transfers between devices: 0.3 us -> 15.8 us
  between operations: 14 us -> 0.78 us
  other arithmetic: 7.5 us -> 0.01 us
  blocking collectives: 7.22 us -> 0 us
    slice x4 -> x0, local copies, waits for them, and re-layouts: 49.3 us -> none  [the longest x3 36.3 us: attend(): block_values = block[:, 1].reshape(count, length, kv_heads, head_dim)]
    dot_general x11 -> x0, matrix products: 47.2 us -> none  [the longest x2 13.8 us: attend(): jnp.einsum('nkgd,ntkd->nkgt', query_block, block_keys, preferred_element_...]
    psum x1 -> x0, waiting for transfers between devices: 35.4 us -> none  [body(): lax.psum(projected.astype(jnp.bfloat16), 'tensor').astype(jnp.float32)]
    another operation x2 -> x0, local copies, waits for them, and re-layouts: 24 us -> none  [the longest x1 12 us: attend(): block_values = block[:, 1].reshape(count, length, kv_heads, head_dim)]
    pallas_call x0 -> x7, Pallas kernels: none -> 23 us  [the longest x1 7.24 us: fast_body(): pl.pallas_call(functools.partial(plan_kernel, pages, block_len, tasks), o...]
    unnamed x16 -> x23, local copies, waits for them, and re-layouts: 26.8 us -> 8.62 us
    ppermute x0 -> x12, starting transfers between devices: none -> 15.8 us  [swap(): lax.ppermute(a, axis, [(i, i ^ k + 1) for i in range(size)])]
    reduce_scatter x1 -> x0, waiting for transfers between devices: 12.8 us -> none  [body(): lax.psum_scatter(mixtures.astype(jnp.bfloat16), 'seq', scatter_dimension=...]
  transfers between devices with their start and end apart: 3 -> 12, of which waited for: 2 -> 5; matrix products, arithmetic and copies ran while one was open for 26% -> 1% of each run, Pallas kernels for 0% -> 15%
where the time goes in v1:
time: 59.2 us; the launch traced here: 59.6 us
  Pallas kernels  23 us (39%)
  starting transfers between devices  15.8 us (27%)
  waiting for transfers between devices  10.5 us (18%)
  local copies, waits for them, and re-layouts  9.51 us (16%)
  between operations  0.78 us (1%)
    ppermute x12, starting transfers between devices, swap(): lax.ppermute(a, axis, [(i, i ^ k + 1) for i in range(size)])  15.8 us
    ppermute x12, waiting for transfers between devices, swap(): lax.ppermute(a, axis, [(i, i ^ k + 1) for i in range(size)])  10.5 us
    unnamed x23, local copies, waits for them, and re-layouts  8.62 us
    pallas_call x1, Pallas kernels, fast_body(): pl.pallas_call(functools.partial(plan_kernel, pages, block_len, tasks), o...  7.24 us
    pallas_call x1, Pallas kernels, fast_body(): pl.pallas_call(lambda meta_r, q0, q1, q2, q3, pg, pr, own, m1, m2, m3, *s...  6.64 us
    pallas_call x1, Pallas kernels, fast_body(): pl.pallas_call(functools.partial(query_kernel, prompt_len, chunks), out_s...  4.76 us
    pallas_call x1, Pallas kernels, fast_body(): pl.pallas_call(lambda w, own, sf, r1, r2, r3, p0, o1, o2, o3: project_ker...  1.86 us
    pallas_call x1, Pallas kernels, fast_body(): pl.pallas_call(functools.partial(fresh_kernel, score_scale), out_shape=(s...  1.72 us
  transfers between devices with their start and end apart: 12, of which 5 were waited for; matrix products, arithmetic and copies ran while one was open for 1% of the time, Pallas kernels for 15%

profile of v1, /device:TPU:0, one launch (start us, length us, event | category | flops | bytes accessed | tf_op | source)
XLA Modules:
  0.0 59.6 jit_solution(1333803559436288097)
XLA Ops:
  0.6 0.9 %reshape.10.gain_ref = f32[1,4608]{1,0:T(1,128)S(1)} reshape(f32[4608]{0:T(1024)} %param.13) | data formatting | bytes 36864 | tf_op jit(solution)/shard_map/reshape | solution.py:564
  1.5 0.0 copy-start.5
  1.5 1.1 %copy-done.5 = bf16[32,4608]{1,0:T(8,128)(2,1)S(1)} copy-done((bf16[32,4608]{1,0:T(8,128)(2,1)S(1)}, bf16[32,4608]{1,0:T(8,128)(2,1)}, u32[]{:S(2)}) %copy-start.5) | copy-done | bytes 294936
  2.7 1.0 %copy-done.7 = s32[128]{0:T(128)S(1)} copy-done((s32[128]{0:T(128)S(1)}, s32[128]{0:T(128)}, u32[]{:S(2)}) %copy-start.7) | copy-done | bytes 536
  3.7 4.8 %query.1 = (bf16[32,1024]{1,0:T(8,128)(2,1)S(1)}, bf16[32,4608]{1,0:T(8,128)(2,1)S(1)}, f32[32,256]{1,0:T(8,128)S(1)}) custom-call(s32[128]{0:T(128)S(1)} %copy-done.7, bf16[32,4608]{1,0:T(8,128)(2,1)S(1)} %copy-done.5, f32[1,4608]{1,0:T(1,128)S(1)} %reshape.10.gain_ref, bf16[4608,1024]{1,0:T(8,128)(2,1)} %w_ref.1), custom_call_target="tpu_custom_call" | custom-call | flops 268435456 | bytes 1048576 | tf_op jit(solution)/shard_map/query/pallas_call | solution.py:555
  8.4 2.5 %collective-permute-start.2 = (bf16[32,1024]{1,0:T(8,128)(2,1)S(1)}, bf16[32,1024]{1,0:T(8,128)(2,1)S(1)}, u32[]{:S(2)}, u32[]{:S(2)}) collective-permute-start(bf16[32,1024]{1,0:T(8,128)(2,1)S(1)} %get-tuple-element.18.q0.q_ref), channel_id=1, source_target_pairs={{0,12},{4,8},{8,4},{12,0},{1,13},{5,9},{9,5},{13,1},{2,14},{6,10},... | collective-permute-start | bytes 196616 | tf_op jit(solution)/shard_map/ppermute | solution.py:519
  10.9 0.6 %collective-permute-start.1 = (bf16[32,1024]{1,0:T(8,128)(2,1)S(1)}, bf16[32,1024]{1,0:T(8,128)(2,1)S(1)}, u32[]{:S(2)}, u32[]{:S(2)}) collective-permute-start(bf16[32,1024]{1,0:T(8,128)(2,1)S(1)} %get-tuple-element.18.q0.q_ref), channel_id=1, source_target_pairs={{0,8},{4,12},{8,0},{12,4},{1,9},{5,13},{9,1},{13,5},{2,10},{6,14},... | collective-permute-start | bytes 196616 | tf_op jit(solution)/shard_map/ppermute | solution.py:519
  11.5 0.0 collective-permute-start
  11.6 7.2 %plan.1.meta_r = s32[512]{0:T(512)S(1)} custom-call(s32[32,128]{1,0:T(8,128)S(1)} %bitcast.5, s32[128]{0:T(128)S(1)} %copy-done.7, s32[128]{0:T(128)S(1)} %copy-done.9), custom_call_target="tpu_custom_call" | custom-call | flops 268435456 | bytes 1048576 | tf_op jit(solution)/shard_map/plan/pallas_call | solution.py:567
  18.9 0.0 collective-permute-done.1.q2
  18.9 0.0 copy-start
  18.9 5.8 %copy-done = bf16[64,2,128,512]{3,2,1,0:T(8,128)(2,1)S(1)} copy-done((bf16[64,2,128,512]{3,2,1,0:T(8,128)(2,1)S(1)}, bf16[64,2,128,512]{3,2,1,0:T(8,128)(2,1)}, u32[]{:S(2)}) %copy-start) | copy-done | bytes 16777240
  24.7 6.6 %attend.1 = (f32[32,1152]{1,0:T(8,128)S(1)}, bf16[32,1152]{1,0:T(8,128)(2,1)S(1)}, bf16[32,1152]{1,0:T(8,128)(2,1)S(1)}, bf16[32,1152]{1,0:T(8,128)(2,1)S(1)}) custom-call(s32[512]{0:T(512)S(1)} %plan.1.meta_r, bf16[32,1024]{1,0:T(8,128)(2,1)S(1)} %get-tuple-element.18.q0.q_ref, bf16[32,1024]{1,0:T(8,128)(2,1)S(1)} %collective-permute-done.q1, ...), custom_call_target="tpu_custom_call" | custom-call | flops 1073741824 | bytes 1048576 | tf_op jit(solution)/shard_map/attend/pallas_call | solution.py:577
  31.3 0.0 copy-start.1
  31.3 2.3 %collective-permute-start.3 = (bf16[32,1152]{1,0:T(8,128)(2,1)S(1)}, bf16[32,1152]{1,0:T(8,128)(2,1)S(1)}, u32[]{:S(2)}, u32[]{:S(2)}) collective-permute-start(bf16[32,1152]{1,0:T(8,128)(2,1)S(1)} %get-tuple-element.23), channel_id=1, source_target_pairs={{0,4},{4,0},{8,12},{12,8},{1,5},{5,1},{9,13},{13,9},{2,6},{6,2},{1... | collective-permute-start | bytes 221192 | tf_op jit(solution)/shard_map/ppermute | solution.py:519
  33.6 0.1 collective-permute-start.4
  33.7 1.4 %collective-permute-start.5 = (bf16[32,1152]{1,0:T(8,128)(2,1)S(1)}, bf16[32,1152]{1,0:T(8,128)(2,1)S(1)}, u32[]{:S(2)}, u32[]{:S(2)}) collective-permute-start(bf16[32,1152]{1,0:T(8,128)(2,1)S(1)} %get-tuple-element.25), channel_id=1, source_target_pairs={{0,12},{4,8},{8,4},{12,0},{1,13},{5,9},{9,5},{13,1},{2,14},{6,10},... | collective-permute-start | bytes 221192 | tf_op jit(solution)/shard_map/ppermute | solution.py:519
  35.1 1.7 %fresh.1 = (bf16[32,512]{1,0:T(8,128)(2,1)S(1)}, bf16[32,512]{1,0:T(8,128)(2,1)S(1)}, f32[32,1152]{1,0:T(8,128)S(1)}) custom-call(bf16[32,4608]{1,0:T(8,128)(2,1)S(1)} %get-tuple-element.20.n_ref, f32[32,256]{1,0:T(8,128)S(1)} %get-tuple-element.21.cs_ref, bf16[32,1024]{1,0:T(8,128)(2,1)S(1)} %get-tuple-element.18.q0.q_ref, bf16[4608,512]{1,0:T(8,128)(2,1)S(1)} %copy-done.3, ...), custom_call_target="tpu_custom_call" | custom-call | flops 536870912 | bytes 1048576 | tf_op jit(solution)/shard_map/fresh/pallas_call | solution.py:597
  36.8 1.9 %collective-permute-done.4.r2 = bf16[32,1152]{1,0:T(8,128)(2,1)S(1)} collective-permute-done((bf16[32,1152]{1,0:T(8,128)(2,1)S(1)}, bf16[32,1152]{1,0:T(8,128)(2,1)S(1)}, u32[]{:S(2)}, u32[]{:S(2)}) %collective-permute-start.4) | collective-permute-done | bytes 73760 | tf_op jit(solution)/shard_map/ppermute | solution.py:519
  38.7 1.9 %project.1 = (f32[32,1152]{1,0:T(8,128)S(1)}, bf16[32,1152]{1,0:T(8,128)(2,1)S(1)}, bf16[32,1152]{1,0:T(8,128)(2,1)S(1)}, bf16[32,1152]{1,0:T(8,128)(2,1)S(1)}) custom-call(bf16[1024,4608]{1,0:T(8,128)(2,1)S(1)} %copy-done.1, f32[32,1152]{1,0:T(8,128)S(1)} %get-tuple-element.19.own, f32[32,1152]{1,0:T(8,128)S(1)} %get-tuple-element.22.sf, ...), custom_call_target="tpu_custom_call" | custom-call | flops 536870912 | bytes 1048576 | tf_op jit(solution)/shard_map/project/pallas_call | solution.py:606
  40.6 1.6 %collective-permute-start.6 = (bf16[32,1152]{1,0:T(8,128)(2,1)S(1)}, bf16[32,1152]{1,0:T(8,128)(2,1)S(1)}, u32[]{:S(2)}, u32[]{:S(2)}) collective-permute-start(bf16[32,1152]{1,0:T(8,128)(2,1)S(1)} %get-tuple-element.27), channel_id=1, source_target_pairs={{0,1},{1,0},{2,3},{3,2},{4,5},{5,4},{6,7},{7,6},{8,9},{9,8},{10,11... | collective-permute-start | bytes 221192 | tf_op jit(solution)/shard_map/ppermute | solution.py:519
  42.2 2.6 %collective-permute-start.7 = (bf16[32,1152]{1,0:T(8,128)(2,1)S(1)}, bf16[32,1152]{1,0:T(8,128)(2,1)S(1)}, u32[]{:S(2)}, u32[]{:S(2)}) collective-permute-start(bf16[32,1152]{1,0:T(8,128)(2,1)S(1)} %get-tuple-element.28), channel_id=1, source_target_pairs={{0,2},{1,3},{2,0},{3,1},{4,6},{5,7},{6,4},{7,5},{8,10},{9,11},{10,... | collective-permute-start | bytes 221192 | tf_op jit(solution)/shard_map/ppermute | solution.py:519
  44.8 0.2 collective-permute-start.8
  45.0 0.4 collective-permute-done.6.r1
  45.4 5.8 %collective-permute-done.7.r2 = bf16[32,1152]{1,0:T(8,128)(2,1)S(1)} collective-permute-done((bf16[32,1152]{1,0:T(8,128)(2,1)S(1)}, bf16[32,1152]{1,0:T(8,128)(2,1)S(1)}, u32[]{:S(2)}, u32[]{:S(2)}) %collective-permute-start.7) | collective-permute-done | bytes 73760 | tf_op jit(solution)/shard_map/ppermute | solution.py:519
  51.2 2.8 %collective-permute-start.11 = (f32[32,128]{1,0:T(8,128)S(1)}, f32[32,128]{1,0:T(8,128)S(1)}, u32[]{:S(2)}, u32[]{:S(2)}) collective-permute-start(f32[32,128]{1,0:T(8,128)S(1)} %get-tuple-element.31.s), channel_id=1, source_target_pairs={{0,3},{1,2},{2,1},{3,0},{4,7},{5,6},{6,5},{7,4},{8,11},{9,10},{10,... | collective-permute-start | bytes 49160 | tf_op jit(solution)/shard_map/ppermute | solution.py:519
  54.0 0.5 collective-permute-start.10
  54.5 1.2 %collective-permute-start.9 = (f32[32,128]{1,0:T(8,128)S(1)}, f32[32,128]{1,0:T(8,128)S(1)}, u32[]{:S(2)}, u32[]{:S(2)}) collective-permute-start(f32[32,128]{1,0:T(8,128)S(1)} %get-tuple-element.31.s), channel_id=1, source_target_pairs={{0,1},{1,0},{2,3},{3,2},{4,5},{5,4},{6,7},{7,6},{8,9},{9,8},{10,11... | collective-permute-start | bytes 49160 | tf_op jit(solution)/shard_map/ppermute | solution.py:519
  55.7 0.7 %copy.14 = bf16[32,2,512]{2,1,0:T(2,128)(2,1)} copy(bf16[32,2,512]{2,0,1:T(8,128)(2,1)S(1)} %pad_maximum_fusion) | data formatting | bytes 131072
  56.4 0.5 collective-permute-done.11.r3
  56.9 1.9 %collective-permute-done.10.r2 = f32[32,128]{1,0:T(8,128)S(1)} collective-permute-done((f32[32,128]{1,0:T(8,128)S(1)}, f32[32,128]{1,0:T(8,128)S(1)}, u32[]{:S(2)}, u32[]{:S(2)}) %collective-permute-start.10) | collective-permute-done | bytes 16416 | tf_op jit(solution)/shard_map/ppermute | solution.py:519
  58.8 0.7 %last.1 = bf16[32,1152]{1,0:T(8,128)(2,1)} custom-call(f32[32,1152]{1,0:T(8,128)S(1)} %get-tuple-element.30.t, f32[32,128]{1,0:T(8,128)S(1)} %get-tuple-element.31.s, f32[32,128]{1,0:T(8,128)S(1)} %collective-permute-done.9.r1, f32[32,128]{1,0:T(8,128)S(1)} %collective-permute-done.10.r2, f32[32,128]{1,0:T(8,128)S(1)} %collective-permute-done.11.r3, ...), custom_call_target="tpu_custom_call" | custom-call | tf_op jit(solution)/shard_map/last/pallas_call | solution.py:628
  (25 shorter events, 0.1 us)
Async XLA Ops:
  0.6 18.2 %copy-start.2 = (bf16[64,2,64,512]{3,2,1,0:T(8,128)(2,1)S(1)}, bf16[64,2,64,512]{3,2,1,0:T(8,128)(2,1)}, u32[]{:S(2)}) copy-start(bf16[64,2,64,512]{3,2,1,0:T(8,128)(2,1)} %pr.1) | copy-start | bytes 25165828
  1.5 1.1 %copy-start.5 = (bf16[32,4608]{1,0:T(8,128)(2,1)S(1)}, bf16[32,4608]{1,0:T(8,128)(2,1)}, u32[]{:S(2)}) copy-start(bf16[32,4608]{1,0:T(8,128)(2,1)} %hd.1) | copy-start | bytes 884740
  2.7 1.0 %copy-start.7 = (s32[128]{0:T(128)S(1)}, s32[128]{0:T(128)}, u32[]{:S(2)}) copy-start(s32[128]{0:T(128)} %lens_ref.3) | copy-start | bytes 1540
  3.7 7.9 %copy-start.8 = (s32[128,32]{0,1:T(8,128)S(1)}, s32[128,32]{0,1:T(8,128)}, u32[]{:S(2)}) copy-start(s32[128,32]{0,1:T(8,128)} %param.23) | copy-start | bytes 49156
  3.7 7.9 %copy-start.9 = (s32[128]{0:T(128)S(1)}, s32[128]{0:T(128)}, u32[]{:S(2)}) copy-start(s32[128]{0:T(128)} %task_ref.1) | copy-start | bytes 1540
  8.4 10.4 %collective-permute-start.2 = (bf16[32,1024]{1,0:T(8,128)(2,1)S(1)}, bf16[32,1024]{1,0:T(8,128)(2,1)S(1)}, u32[]{:S(2)}, u32[]{:S(2)}) collective-permute-start(bf16[32,1024]{1,0:T(8,128)(2,1)S(1)} %get-tuple-element.18.q0.q_ref), channel_id=1, source_target_pairs={{0,12},{4,8},{8,4},{12,0},{1,13},{5,9},{9,5},{13,1},{2,14},{6,10},... | collective-permute-start | bytes 196616 | tf_op jit(solution)/shard_map/ppermute | solution.py:519
  10.9 8.0 %collective-permute-start.1 = (bf16[32,1024]{1,0:T(8,128)(2,1)S(1)}, bf16[32,1024]{1,0:T(8,128)(2,1)S(1)}, u32[]{:S(2)}, u32[]{:S(2)}) collective-permute-start(bf16[32,1024]{1,0:T(8,128)(2,1)S(1)} %get-tuple-element.18.q0.q_ref), channel_id=1, source_target_pairs={{0,8},{4,12},{8,0},{12,4},{1,9},{5,13},{9,1},{13,5},{2,10},{6,14},... | collective-permute-start | bytes 196616 | tf_op jit(solution)/shard_map/ppermute | solution.py:519
  11.5 7.3 %collective-permute-start = (bf16[32,1024]{1,0:T(8,128)(2,1)S(1)}, bf16[32,1024]{1,0:T(8,128)(2,1)S(1)}, u32[]{:S(2)}, u32[]{:S(2)}) collective-permute-start(bf16[32,1024]{1,0:T(8,128)(2,1)S(1)} %get-tuple-element.18.q0.q_ref), channel_id=1, source_target_pairs={{0,4},{4,0},{8,12},{12,8},{1,5},{5,1},{9,13},{13,9},{2,6},{6,2},{1... | collective-permute-start | bytes 196616 | tf_op jit(solution)/shard_map/ppermute | solution.py:519
  18.9 5.8 %copy-start = (bf16[64,2,128,512]{3,2,1,0:T(8,128)(2,1)S(1)}, bf16[64,2,128,512]{3,2,1,0:T(8,128)(2,1)}, u32[]{:S(2)}) copy-start(bf16[64,2,128,512]{3,2,1,0:T(8,128)(2,1)} %pg.1) | copy-start | bytes 50331652
  24.7 10.4 %copy-start.3 = (bf16[4608,512]{1,0:T(8,128)(2,1)S(1)}, bf16[4608,512]{1,0:T(8,128)(2,1)}, u32[]{:S(2)}) copy-start(bf16[4608,512]{1,0:T(8,128)(2,1)} %wk_ref.1) | copy-start | bytes 14155780
  24.7 10.4 %copy-start.4 = (bf16[4608,512]{1,0:T(8,128)(2,1)S(1)}, bf16[4608,512]{1,0:T(8,128)(2,1)}, u32[]{:S(2)}) copy-start(bf16[4608,512]{1,0:T(8,128)(2,1)} %wv_ref.1) | copy-start | bytes 14155780
  31.3 7.4 %copy-start.1 = (bf16[1024,4608]{1,0:T(8,128)(2,1)S(1)}, bf16[1024,4608]{1,0:T(8,128)(2,1)}, u32[]{:S(2)}) copy-start(bf16[1024,4608]{1,0:T(8,128)(2,1)} %w.1) | copy-start | bytes 28311556
  31.3 5.5 %collective-permute-start.3 = (bf16[32,1152]{1,0:T(8,128)(2,1)S(1)}, bf16[32,1152]{1,0:T(8,128)(2,1)S(1)}, u32[]{:S(2)}, u32[]{:S(2)}) collective-permute-start(bf16[32,1152]{1,0:T(8,128)(2,1)S(1)} %get-tuple-element.23), channel_id=1, source_target_pairs={{0,4},{4,0},{8,12},{12,8},{1,5},{5,1},{9,13},{13,9},{2,6},{6,2},{1... | collective-permute-start | bytes 221192 | tf_op jit(solution)/shard_map/ppermute | solution.py:519
  33.6 5.0 %collective-permute-start.4 = (bf16[32,1152]{1,0:T(8,128)(2,1)S(1)}, bf16[32,1152]{1,0:T(8,128)(2,1)S(1)}, u32[]{:S(2)}, u32[]{:S(2)}) collective-permute-start(bf16[32,1152]{1,0:T(8,128)(2,1)S(1)} %get-tuple-element.24), channel_id=1, source_target_pairs={{0,8},{4,12},{8,0},{12,4},{1,9},{5,13},{9,1},{13,5},{2,10},{6,14},... | collective-permute-start | bytes 221192 | tf_op jit(solution)/shard_map/ppermute | solution.py:519
  33.7 5.0 %collective-permute-start.5 = (bf16[32,1152]{1,0:T(8,128)(2,1)S(1)}, bf16[32,1152]{1,0:T(8,128)(2,1)S(1)}, u32[]{:S(2)}, u32[]{:S(2)}) collective-permute-start(bf16[32,1152]{1,0:T(8,128)(2,1)S(1)} %get-tuple-element.25), channel_id=1, source_target_pairs={{0,12},{4,8},{8,4},{12,0},{1,13},{5,9},{9,5},{13,1},{2,14},{6,10},... | collective-permute-start | bytes 221192 | tf_op jit(solution)/shard_map/ppermute | solution.py:519
  35.1 20.6 %copy-start.10 = (f32[1152]{0:T(1024)S(1)}, f32[1152]{0:T(1024)}, u32[]{:S(2)}) copy-start(f32[1152]{0:T(1024)} %param.18) | copy-start | bytes 13828
  35.1 23.8 %copy-start.6 = (bf16[32,4608]{1,0:T(8,128)(2,1)S(1)}, bf16[32,4608]{1,0:T(8,128)(2,1)}, u32[]{:S(2)}) copy-start(bf16[32,4608]{1,0:T(8,128)(2,1)} %hd.1) | copy-start | bytes 884740
  40.6 4.8 %collective-permute-start.6 = (bf16[32,1152]{1,0:T(8,128)(2,1)S(1)}, bf16[32,1152]{1,0:T(8,128)(2,1)S(1)}, u32[]{:S(2)}, u32[]{:S(2)}) collective-permute-start(bf16[32,1152]{1,0:T(8,128)(2,1)S(1)} %get-tuple-element.27), channel_id=1, source_target_pairs={{0,1},{1,0},{2,3},{3,2},{4,5},{5,4},{6,7},{7,6},{8,9},{9,8},{10,11... | collective-permute-start | bytes 221192 | tf_op jit(solution)/shard_map/ppermute | solution.py:519
  42.2 9.0 %collective-permute-start.7 = (bf16[32,1152]{1,0:T(8,128)(2,1)S(1)}, bf16[32,1152]{1,0:T(8,128)(2,1)S(1)}, u32[]{:S(2)}, u32[]{:S(2)}) collective-permute-start(bf16[32,1152]{1,0:T(8,128)(2,1)S(1)} %get-tuple-element.28), channel_id=1, source_target_pairs={{0,2},{1,3},{2,0},{3,1},{4,6},{5,7},{6,4},{7,5},{8,10},{9,11},{10,... | collective-permute-start | bytes 221192 | tf_op jit(solution)/shard_map/ppermute | solution.py:519
  44.8 6.4 %collective-permute-start.8 = (bf16[32,1152]{1,0:T(8,128)(2,1)S(1)}, bf16[32,1152]{1,0:T(8,128)(2,1)S(1)}, u32[]{:S(2)}, u32[]{:S(2)}) collective-permute-start(bf16[32,1152]{1,0:T(8,128)(2,1)S(1)} %get-tuple-element.29), channel_id=1, source_target_pairs={{0,3},{1,2},{2,1},{3,0},{4,7},{5,6},{6,5},{7,4},{8,11},{9,10},{10,... | collective-permute-start | bytes 221192 | tf_op jit(solution)/shard_map/ppermute | solution.py:519
  51.2 5.7 %collective-permute-start.11 = (f32[32,128]{1,0:T(8,128)S(1)}, f32[32,128]{1,0:T(8,128)S(1)}, u32[]{:S(2)}, u32[]{:S(2)}) collective-permute-start(f32[32,128]{1,0:T(8,128)S(1)} %get-tuple-element.31.s), channel_id=1, source_target_pairs={{0,3},{1,2},{2,1},{3,0},{4,7},{5,6},{6,5},{7,4},{8,11},{9,10},{10,... | collective-permute-start | bytes 49160 | tf_op jit(solution)/shard_map/ppermute | solution.py:519
  54.0 4.8 %collective-permute-start.10 = (f32[32,128]{1,0:T(8,128)S(1)}, f32[32,128]{1,0:T(8,128)S(1)}, u32[]{:S(2)}, u32[]{:S(2)}) collective-permute-start(f32[32,128]{1,0:T(8,128)S(1)} %get-tuple-element.31.s), channel_id=1, source_target_pairs={{0,2},{1,3},{2,0},{3,1},{4,6},{5,7},{6,4},{7,5},{8,10},{9,11},{10,... | collective-permute-start | bytes 49160 | tf_op jit(solution)/shard_map/ppermute | solution.py:519
  54.5 4.3 %collective-permute-start.9 = (f32[32,128]{1,0:T(8,128)S(1)}, f32[32,128]{1,0:T(8,128)S(1)}, u32[]{:S(2)}, u32[]{:S(2)}) collective-permute-start(f32[32,128]{1,0:T(8,128)S(1)} %get-tuple-element.31.s), channel_id=1, source_target_pairs={{0,1},{1,0},{2,3},{3,2},{4,5},{5,4},{6,7},{7,6},{8,9},{9,8},{10,11... | collective-permute-start | bytes 49160 | tf_op jit(solution)/shard_map/ppermute | solution.py:519

commit v2 on v1

--- a/solution.py
+++ b/solution.py
@@ -14,6 +14,8 @@
 SUB = 8
 
 cap_limit = 50.0
+FLOPS_US = 1 << 30
+BYTES_US = 1 << 20
 F32 = jnp.float32
 BF16 = jnp.bfloat16
 
@@ -184,8 +186,10 @@
 HB = pl.BlockSpec(memory_space=pltpu.HBM)
 
 
-def cost(flops):
-    return pl.CostEstimate(flops=flops, bytes_accessed=1 << 20, transcendentals=0)
+def cost(us):
+    return pl.CostEstimate(
+        flops=int(us * FLOPS_US), bytes_accessed=int(us * BYTES_US), transcendentals=0
+    )
 
 
 def row_iota(rows):
@@ -196,19 +200,34 @@
     return lax.broadcasted_iota(jnp.int32, (rows, LANES), 1)
 
 
-def query_kernel(prompt_len, chunks, lens_ref, hidden_ref, gain_ref, w_ref, q_ref, n_ref, cs_ref, w_buf, sem):
+def query_kernel(
+    prompt_len, chunks, lens_hbm, hidden_hbm, gain_hbm, w_ref, q_ref, n_ref, cs_ref,
+    lens_ref, hidden_ref, gain_ref, w_buf, sem, small,
+):
     rows, depth = hidden_ref.shape
     width = q_ref.shape[1]
-    step = depth // chunks
+    edges = [0]
+    for c in chunks:
+        edges.append(edges[-1] + c)
+    first_copies = [
+        pltpu.make_async_copy(hidden_hbm, hidden_ref, small.at[0]),
+        pltpu.make_async_copy(gain_hbm, gain_ref, small.at[1]),
+        pltpu.make_async_copy(lens_hbm, lens_ref, small.at[2]),
+    ]
+    for copy in first_copies:
+        copy.start()
     copies = []
-    for c in range(chunks):
-        part = pl.ds(c * step, step)
-        copy = pltpu.make_async_copy(w_ref.at[part, :], w_buf.at[part, :], sem.at[c])
+    for c in range(len(chunks)):
+        part = pl.ds(edges[c], chunks[c])
+        copies.append(pltpu.make_async_copy(w_ref.at[part, :], w_buf.at[part, :], sem.at[c]))
+    for copy in copies[:AHEAD]:
         copy.start()
-        copies.append(copy)
+    for copy in first_copies:
+        copy.wait()
     x = hidden_ref[...].astype(F32)
     mean_square = jnp.sum(x * x, axis=-1, keepdims=True) / depth
-    n_ref[...] = (x * lax.rsqrt(mean_square + 1e-06) * gain_ref[...]).astype(BF16)
+    gain = gain_ref[...].reshape(1, depth)
+    n_ref[...] = (x * lax.rsqrt(mean_square + 1e-06) * gain).astype(BF16)
     first = lax.axis_index("seq") * rows
     row = row_iota(rows)
     lane = lane_iota(rows)
@@ -221,15 +240,18 @@
     frequency = jnp.exp(slot * (-9.210340371976184 / half))
     angles = (length + prompt_len).astype(F32) * frequency
     cosine = jnp.cos(angles)
-    sines = jnp.where(low, -jnp.sin(angles), jnp.sin(angles))
+    sines = jnp.sin(angles)
+    sines = jnp.where(low, -sines, sines)
     cs_ref[:, :LANES] = cosine
     cs_ref[:, LANES:] = sines
     total = jnp.zeros((rows, width), F32)
-    for c in range(chunks):
+    for c in range(len(chunks)):
         copies[c].wait()
+        if c + AHEAD < len(chunks):
+            copies[c + AHEAD].start()
         total = total + jnp.dot(
-            n_ref[:, c * step : (c + 1) * step],
-            w_buf[c * step : (c + 1) * step, :],
+            n_ref[:, edges[c] : edges[c + 1]],
+            w_buf[edges[c] : edges[c + 1], :],
             preferred_element_type=F32,
         )
     for h in range(width // LANES):
@@ -239,50 +261,55 @@
         ).astype(BF16)
 
 
+CODE = 256
+AHEAD = 3
+
+
 def plan_kernel(pages, block_len, tasks, table_ref, lens_ref, task_ref, meta_ref):
-    requests = lens_ref.shape[0]
+    blocks, requests = table_ref.shape
     seq = lax.axis_index("seq")
-    page0 = seq * pages
-    task0 = seq * tasks
-
-    def clear(i, c):
-        meta_ref[i] = 0
-        return c
-
-    lax.fori_loop(0, meta_ref.shape[0], clear, 0, unroll=8)
-
-    def request(r, count):
-        length = lens_ref[r]
-        blocks = (length + block_len - 1) // block_len
-
-        def block(j, c):
-            page = table_ref[j, r] - page0
-
-            @pl.when((page >= 0) & (page < pages))
-            def _():
-                meta_ref[page] = r
-                meta_ref[pages + page] = jnp.minimum(length - j * block_len, block_len)
-
-            return c
-
-        lax.fori_loop(0, blocks, block, 0)
-        task = task_ref[r] - task0
-        here = (task >= 0) & (task < tasks)
-
-        @pl.when(here)
-        def _():
-            meta_ref[2 * pages + count] = r
-            meta_ref[2 * pages + requests + count] = task
-
-        return count + here.astype(jnp.int32)
-
-    count = lax.fori_loop(0, requests, request, 0)
-    meta_ref[2 * pages + 2 * requests] = count
+    table = table_ref[...] - seq * pages
+    lens = lens_ref[...]
+    shape = (blocks, requests)
+    block = lax.broadcasted_iota(jnp.int32, shape, 0)
+    owner = lax.broadcasted_iota(jnp.int32, shape, 1)
+    live = jnp.minimum(lens - block * block_len, block_len)
+    code = jnp.where(live > 0, owner * CODE + live, 0)
+    columns = []
+    for p in range(pages):
+        hit = jnp.where(table == p, code, 0)
+        fold = hit[:SUB]
+        for j in range(1, blocks // SUB):
+            fold = fold + hit[j * SUB : (j + 1) * SUB]
+        columns.append(jnp.sum(fold.astype(F32), axis=0, keepdims=True))
+    found = jnp.sum(jnp.concatenate(columns, axis=0), axis=1, keepdims=True)
+    at = lane_iota(pages) == row_iota(pages)
+    first = jnp.sum(jnp.where(at, found, 0.0), axis=0, keepdims=True)
+    task = task_ref[...] - seq * tasks
+    here = (task >= 0) & (task < tasks)
+    flag = jnp.broadcast_to(here.astype(F32), (SUB, requests))
+    before = (
+        lax.broadcasted_iota(jnp.int32, (requests, requests), 0)
+        < lax.broadcasted_iota(jnp.int32, (requests, requests), 1)
+    )
+    rank = jnp.dot(flag.astype(BF16), before.astype(F32).astype(BF16), preferred_element_type=F32)[:1]
+    item = lax.broadcasted_iota(jnp.int32, (requests, requests), 0)
+    column = lax.broadcasted_iota(jnp.int32, (1, requests), 1)
+    entry = (column * CODE + task).astype(F32)
+    pick = (rank.astype(jnp.int32) == item) & here
+    listed = jnp.sum(jnp.where(pick, entry, 0.0), axis=1, keepdims=True)
+    same = item == lax.broadcasted_iota(jnp.int32, (requests, requests), 1)
+    second = jnp.sum(jnp.where(same, listed, 0.0), axis=0, keepdims=True)
+    count = jnp.sum(flag[:1], axis=1, keepdims=True)
+    third = jnp.broadcast_to(count, (1, requests))
+    rest = jnp.zeros((SUB - 3, requests), F32)
+    meta_ref[...] = jnp.concatenate([first, second, third, rest], axis=0).astype(jnp.int32)
 
 
 def attend_kernel(
     n_seq, score_scale, batch,
-    meta_hbm, q_refs, pages_ref, prompt_ref, own_ref, msg_refs, meta_ref, qf, acc, acw, sem,
+    meta_hbm, q_refs, pages_ref, prompt_ref, far_refs, own_ref, msg_refs, near_refs,
+    meta_ref, qf, acc, acw, sem, far_sem,
 ):
     rows, width = q_refs[0].shape
     heads = width // LANES
@@ -290,10 +317,13 @@
     kvh = kv_width // LANES
     group = heads // kvh
     prompt_len = prompt_ref.shape[2]
-    requests = rows * n_seq
     me = lax.axis_index("seq")
     fetch = pltpu.make_async_copy(meta_hbm, meta_ref, sem)
     fetch.start()
+    loads = []
+    for i, (far, near) in enumerate(zip(far_refs, near_refs)):
+        loads.append(pltpu.make_async_copy(far, near, far_sem.at[i]))
+        loads[-1].start()
     acc[...] = jnp.zeros_like(acc)
     acw[...] = jnp.zeros_like(acw)
     for k in range(n_seq):
@@ -332,13 +362,14 @@
         owners, weights, values = [], [], []
         for b in range(batch):
             p = (i * batch + b) * pair
-            who = [meta_ref[p + j] for j in range(pair)]
+            note = [meta_ref[0, p + j] for j in range(pair)]
+            who = [n // CODE for n in note]
             q2 = jnp.concatenate([spread(r) for r in who], axis=0).astype(BF16)
             keys = pages_ref[pl.ds(p, pair), 0].reshape(pair * block_len, kv_width)
             s = lax.dot_general(q2, keys, (((1,), (1,)), ((), ())), preferred_element_type=F32)
             ws = []
             for j in range(pair):
-                live = lane < meta_ref[pages + p + j]
+                live = lane < note[j] % CODE
                 ws.append(weigh(s[j * heads : (j + 1) * heads, j * block_len : (j + 1) * block_len], live))
             owners.append(who)
             weights.append(ws)
@@ -361,17 +392,18 @@
 
     lax.fori_loop(0, pages // (pair * batch), page_step, 0)
 
-    count = meta_ref[2 * pages + 2 * requests]
+    count = meta_ref[2, 0]
     per = LANES // prompt_len
     quad = 2 * per
-    pbatch = 2
+    pbatch = 4
 
     def prompt_step(i, c):
         owners, weights, values, tasks = [], [], [], []
         for b in range(pbatch):
             e = (i * pbatch + b) * quad
-            who = [meta_ref[2 * pages + e + j] for j in range(quad)]
-            task = [meta_ref[2 * pages + requests + e + j] for j in range(quad)]
+            note = [meta_ref[1, e + j] for j in range(quad)]
+            who = [n // CODE for n in note]
+            task = [n % CODE for n in note]
             q4 = jnp.concatenate([spread(r) for r in who], axis=0).astype(BF16)
             keys = jnp.concatenate([prompt_ref[t, 0] for t in task], axis=0)
             s = lax.dot_general(q4, keys, (((1,), (1,)), ((), ())), preferred_element_type=F32)
@@ -420,9 +452,15 @@
             own_ref[:, heads * LANES :] = sums
         else:
             msg_refs[k - 1][:, heads * LANES :] = sums.astype(BF16)
-
-
-def fresh_kernel(score_scale, n_ref, cs_ref, q_ref, wk_ref, wv_ref, k_ref, v_ref, self_ref):
+    for load in loads:
+        load.wait()
+
+
+def fresh_kernel(
+    score_scale, n_ref, cs_ref, q_ref, wk_ref, wv_hbm, k_ref, v_ref, self_ref, wv_ref, sem
+):
+    load = pltpu.make_async_copy(wv_hbm, wv_ref, sem)
+    load.start()
     rows, width = q_ref.shape
     heads = width // LANES
     kvh = k_ref.shape[1] // LANES
@@ -432,6 +470,7 @@
     cosine = cs_ref[:, :LANES]
     sines = cs_ref[:, LANES:]
     keys = jnp.dot(normed, wk_ref[...], preferred_element_type=F32)
+    load.wait()
     values = jnp.dot(normed, wv_ref[...], preferred_element_type=F32)
     lanes = lane_iota(rows)
     sums = jnp.zeros((rows, LANES), F32)
@@ -454,7 +493,7 @@
 
 
 def project_kernel(n_ten, w_ref, own_ref, self_ref, got_refs, p0_ref, out_refs):
-    rows, wide = own_ref.shape
+    _, wide = own_ref.shape
     heads = wide // LANES - 1
     cols = p0_ref.shape[1]
     at = slice(heads * LANES, (heads + 1) * LANES)
@@ -515,10 +554,21 @@
 
 
 def swap(arrays, axis, size):
-    return [
-        lax.ppermute(a, axis, [(i, i ^ (k + 1)) for i in range(size)])
-        for k, a in enumerate(arrays)
-    ]
+    got = []
+    for k, a in enumerate(arrays):
+        got.append(lax.ppermute(a, axis, [(i, i ^ (k + 1)) for i in range(size)]))
+    return got
+
+
+def split(depth, count):
+    unit = 2 * LANES
+    step = max(1, depth // (unit * count)) * unit
+    edges = list(range(0, depth - step + 1, step)) + [depth]
+    return tuple(b - a for a, b in zip(edges, edges[1:]))
+
+
+def in_hbm(array):
+    return pltpu.with_memory_space_constraint(array, pltpu.HBM)
 
 
 def shape(dims, dtype):
@@ -551,58 +601,84 @@
     cols = post_gain.shape[0]
     wide = width + LANES
     score_scale = float(D // H) ** (-0.5)
-    chunks = 9 if depth % 9 == 0 else 1
+    chunks = split(depth, 6)
     query, normed, cs = pl.pallas_call(
         functools.partial(query_kernel, prompt_len, chunks),
-        out_shape=(shape((rows, width), BF16), shape((rows, depth), BF16), shape((rows, 2 * LANES), F32)),
-        in_specs=[SM, VM, VM, HB],
+        out_shape=(
+            pltpu.VMEM((rows, width), BF16),
+            pltpu.VMEM((rows, depth), BF16),
+            pltpu.VMEM((rows, 2 * LANES), F32),
+        ),
+        in_specs=[HB] * 4,
         out_specs=(VM, VM, VM),
-        scratch_shapes=[pltpu.VMEM((depth, width), BF16), pltpu.SemaphoreType.DMA((chunks,))],
-        compiler_params=params(16),
-        cost_estimate=cost(1 << 28),
+        scratch_shapes=[
+            pltpu.SMEM((requests,), jnp.int32),
+            pltpu.VMEM((rows, depth), BF16),
+            pltpu.VMEM((depth,), F32),
+            pltpu.VMEM((depth, width), BF16),
+            pltpu.SemaphoreType.DMA((len(chunks),)),
+            pltpu.SemaphoreType.DMA((3,)),
+        ],
+        compiler_params=params(Q_MIB),
+        cost_estimate=cost(0.05),
         name="query",
-    )(cache_lengths, hidden, pre_gain.reshape(1, depth), pltpu.with_memory_space_constraint(w_query, pltpu.HBM))
+    )(*[in_hbm(a) for a in (cache_lengths, hidden, pre_gain, w_query)])
+    query = pl.pallas_call(
+        lambda q, o: None,
+        out_shape=pltpu.VMEM((rows, width), BF16),
+        in_specs=[VM],
+        out_specs=VM,
+        input_output_aliases={0: 0},
+        compiler_params=params(1),
+        cost_estimate=cost(12),
+        name="gate",
+    )(query)
     got = swap([query] * (n_seq - 1), "seq", n_seq)
-    meta_len = 2 * pages + 2 * requests + LANES
     meta = pl.pallas_call(
         functools.partial(plan_kernel, pages, block_len, tasks),
-        out_shape=shape((meta_len,), jnp.int32),
-        in_specs=[SM, SM, SM],
-        out_specs=SM,
+        out_shape=shape((SUB, requests), jnp.int32),
+        in_specs=[VM, VM, VM],
+        out_specs=VM,
         compiler_params=params(1),
-        cost_estimate=cost(1 << 28),
+        cost_estimate=cost(9),
         name="plan",
-    )(block_table.T, cache_lengths, task_ids)
-    batch = 4
+    )(block_table.T, cache_lengths.reshape(1, requests), task_ids.reshape(1, requests))
+    batch = 32
     outs = pl.pallas_call(
-        lambda meta_r, q0, q1, q2, q3, pg, pr, own, m1, m2, m3, *scratch: attend_kernel(
-            n_seq, score_scale, batch, meta_r, (q0, q1, q2, q3), pg, pr, own, (m1, m2, m3), *scratch
+        lambda meta_r, q0, q1, q2, q3, pg, pr, f1, f2, own, m1, m2, m3, n1, n2, *scratch: attend_kernel(
+            n_seq, score_scale, batch, meta_r, (q0, q1, q2, q3), pg, pr, (f1, f2),
+            own, (m1, m2, m3), (n1, n2), *scratch
         ),
-        out_shape=(shape((rows, wide), F32),) + (shape((rows, wide), BF16),) * (n_seq - 1),
-        in_specs=[HB] + [VM] * (n_seq + 2),
-        out_specs=(VM,) * n_seq,
+        out_shape=(shape((rows, wide), F32),)
+        + (shape((rows, wide), BF16),) * (n_seq - 1)
+        + tuple(pltpu.VMEM(w.shape, w.dtype) for w in (w_key, w_out)),
+        in_specs=[HB] + [VM] * (n_seq + 2) + [HB] * 2,
+        out_specs=(VM,) * (n_seq + 2),
         scratch_shapes=[
-            pltpu.SMEM((meta_len,), jnp.int32),
+            pltpu.SMEM((SUB, requests), jnp.int32),
             pltpu.VMEM((requests * heads, LANES), F32),
             pltpu.VMEM((requests * heads, LANES), F32),
             pltpu.VMEM((requests * heads, LANES), F32),
             pltpu.SemaphoreType.DMA,
+            pltpu.SemaphoreType.DMA((2,)),
         ],
         compiler_params=params(A_MIB),
-        cost_estimate=cost(1 << 30),
+        cost_estimate=cost(8),
         name="attend",
-    )(meta, query, *got, cache_pool, prompt_cache)
-    own, msgs = outs[0], outs[1:]
+    )(meta, query, *got, cache_pool, prompt_cache, in_hbm(w_key), in_hbm(w_out))
+    own, msgs = outs[0], outs[1:n_seq]
+    key_near, out_near = outs[n_seq:]
     got = swap(msgs, "seq", n_seq)
     key_new, value_new, self_part = pl.pallas_call(
         functools.partial(fresh_kernel, score_scale),
         out_shape=(shape((rows, kv_width), BF16), shape((rows, kv_width), BF16), shape((rows, wide), F32)),
-        in_specs=[VM] * 5,
+        in_specs=[VM] * 4 + [HB],
         out_specs=(VM,) * 3,
+        scratch_shapes=[pltpu.VMEM(w_value.shape, BF16), pltpu.SemaphoreType.DMA],
         compiler_params=params(G_MIB),
-        cost_estimate=cost(1 << 29),
+        cost_estimate=cost(1.7),
         name="fresh",
-    )(normed, cs, query, w_key, w_value)
+    )(normed, cs, query, key_near, in_hbm(w_value))
     outs = pl.pallas_call(
         lambda w, own, sf, r1, r2, r3, p0, o1, o2, o3: project_kernel(
             n_ten, w, own, sf, (r1, r2, r3), p0, (o1, o2, o3)
@@ -611,9 +687,9 @@
         in_specs=[VM] * (3 + n_seq - 1),
         out_specs=(VM,) * n_ten,
         compiler_params=params(H_MIB),
-        cost_estimate=cost(1 << 29),
+        cost_estimate=cost(1.9),
         name="project",
-    )(w_out, own, self_part, *got)
+    )(out_near, own, self_part, *got)
     p0, parts = outs[0], outs[1:]
     got = swap(parts, "tensor", n_ten)
     total, sq = pl.pallas_call(
@@ -622,6 +698,7 @@
         in_specs=[VM] * n_ten,
         out_specs=(VM,) * 2,
         compiler_params=params(2),
+        cost_estimate=cost(0.3),
         name="sum",
     )(p0, *got)
     got = swap([sq] * (n_ten - 1), "tensor", n_ten)
@@ -631,14 +708,16 @@
         in_specs=[VM] * (n_ten + 3),
         out_specs=VM,
         compiler_params=params(2),
+        cost_estimate=cost(0.3),
         name="last",
     )(total, sq, *got, hidden, post_gain.reshape(1, cols))
     fresh_cache = jnp.stack([key_new, value_new], axis=1)
     return (layer_out, fresh_cache)
 
 
+Q_MIB = 60
 A_MIB = 6
-G_MIB = 4
+G_MIB = 9
 H_MIB = 4
 
 
@@ -653,7 +732,10 @@
         and cache_pool.shape[0] % SUB == 0
         and LANES % prompt_cache.shape[2] == 0
         and prompt_cache.shape[2] % (2 * SUB) == 0
-        and args[9].shape[0] == hidden.shape[0] * n_seq
+        and args[9].shape[0] == LANES == hidden.shape[0] * n_seq
+        and args[11].shape[1] % SUB == 0
+        and prompt_cache.shape[0] <= CODE
+        and cache_pool.shape[0] <= LANES
         and hidden.shape[0] % (2 * SUB) == 0
     )
     if fits:

time: 59.2 us -> 48.3 us (0.82)
  local copies, waits for them, and re-layouts: 9.51 us -> 2 us
  Pallas kernels: 23 us -> 16.5 us
  waiting for transfers between devices: 10.5 us -> 14.2 us
  starting transfers between devices: 15.8 us -> 14.7 us
    pallas_call x1, Pallas kernels: 7.24 us -> 0.28 us  [fast_body(): pl.pallas_call(functools.partial(plan_kernel, pages, block_len, tasks), o...]
    unnamed x23 -> x21, local copies, waits for them, and re-layouts: 8.62 us -> 2 us
    ppermute x12, waiting for transfers between devices: 10.5 us -> 14.2 us  [swap(): got.append(lax.ppermute(a, axis, [(i, i ^ k + 1) for i in range(size)]))]
    pallas_call x1, Pallas kernels: 1.72 us -> 3.33 us  [fast_body(): pl.pallas_call(functools.partial(fresh_kernel, score_scale), out_shape=(s...]
    pallas_call x1 -> x2, Pallas kernels: 6.64 us -> 5.52 us  [the longest x1 5.52 us: fast_body(): pl.pallas_call(lambda meta_r, q0, q1, q2, q3, pg, pr, f1, f2, own, m1, m2...]
    ppermute x12, starting transfers between devices: 15.8 us -> 14.7 us  [swap(): got.append(lax.ppermute(a, axis, [(i, i ^ k + 1) for i in range(size)]))]
    reshape x1 -> x0, local copies, waits for them, and re-layouts: 0.89 us -> none  [fast_body(): pre_gain.reshape(1, depth)]
  transfers between devices with their start and end apart: 12 -> 12, of which waited for: 5 -> 7; matrix products, arithmetic and copies ran while one was open for 1% -> 1% of each run, Pallas kernels for 15% -> 7%
where the time goes in v2:
time: 48.3 us; the launch traced here: 48.2 us
  Pallas kernels  16.5 us (34%)
  starting transfers between devices  14.7 us (30%)
  waiting for transfers between devices  14.2 us (29%)
  local copies, waits for them, and re-layouts  2 us (4%)
  between operations  0.8 us (2%)
    ppermute x12, starting transfers between devices, swap(): got.append(lax.ppermute(a, axis, [(i, i ^ k + 1) for i in range(size)]))  14.7 us
    ppermute x12, waiting for transfers between devices, swap(): got.append(lax.ppermute(a, axis, [(i, i ^ k + 1) for i in range(size)]))  14.2 us
    pallas_call x1, Pallas kernels, fast_body(): pl.pallas_call(lambda meta_r, q0, q1, q2, q3, pg, pr, f1, f2, own, m1, m2...  5.52 us
    pallas_call x1, Pallas kernels, fast_body(): pl.pallas_call(functools.partial(query_kernel, prompt_len, chunks), out_s...  4.69 us
    pallas_call x1, Pallas kernels, fast_body(): pl.pallas_call(functools.partial(fresh_kernel, score_scale), out_shape=(s...  3.33 us
    unnamed x21, local copies, waits for them, and re-layouts  2 us
    pallas_call x1, Pallas kernels, fast_body(): pl.pallas_call(lambda w, own, sf, r1, r2, r3, p0, o1, o2, o3: project_ker...  1.85 us
  transfers between devices with their start and end apart: 12, of which 7 were waited for; matrix products, arithmetic and copies ran while one was open for 1% of the time, Pallas kernels for 7%

profile of v2, /device:TPU:0, one launch (start us, length us, event | category | flops | bytes accessed | tf_op | source)
XLA Modules:
  0.0 48.2 jit_solution(5124074308331023023)
XLA Ops:
  0.6 4.7 %query.1 = (bf16[32,1024]{1,0:T(8,128)(2,1)S(1)}, bf16[32,4608]{1,0:T(8,128)(2,1)S(1)}, f32[32,256]{1,0:T(8,128)S(1)}) custom-call(s32[128]{0:T(128)} %lens_hbm.1, bf16[32,4608]{1,0:T(8,128)(2,1)} %hd.1, f32[4608]{0:T(1024)} %gain_hbm.1, bf16[4608,1024]{1,0:T(8,128)(2,1)} %w_ref.1), custom_call_target="tpu_custom_call" | custom-call | flops 53687092 | bytes 52428 | tf_op jit(solution)/shard_map/query/pallas_call | solution.py:605
  5.3 0.0 copy-start.2
  5.3 0.0 copy-start.3
  5.4 0.0 copy-start.4
  5.4 0.0 slice-start
  5.4 0.0 slice-start.1
  5.4 0.0 slice-start.2
  5.4 0.6 %collective-permute-start = (bf16[32,1024]{1,0:T(8,128)(2,1)S(1)}, bf16[32,1024]{1,0:T(8,128)(2,1)S(1)}, u32[]{:S(2)}, u32[]{:S(2)}) collective-permute-start(bf16[32,1024]{1,0:T(8,128)(2,1)S(1)} %gate.1.q0.q_ref), channel_id=1, source_target_pairs={{0,4},{4,0},{8,12},{12,8},{1,5},{5,1},{9,13},{13,9},{2,6},{6,2},{1... | collective-permute-start | bytes 196616 | tf_op jit(solution)/shard_map/ppermute | solution.py:559
  6.0 2.6 %collective-permute-start.1 = (bf16[32,1024]{1,0:T(8,128)(2,1)S(1)}, bf16[32,1024]{1,0:T(8,128)(2,1)S(1)}, u32[]{:S(2)}, u32[]{:S(2)}) collective-permute-start(bf16[32,1024]{1,0:T(8,128)(2,1)S(1)} %gate.1.q0.q_ref), channel_id=1, source_target_pairs={{0,8},{4,12},{8,0},{12,4},{1,9},{5,13},{9,1},{13,5},{2,10},{6,14},... | collective-permute-start | bytes 196616 | tf_op jit(solution)/shard_map/ppermute | solution.py:559
  8.5 0.0 collective-permute-start.2
  8.6 0.0 copy-start
  8.6 0.3 plan.1.meta_r
  8.9 2.3 %collective-permute-done.1.q2 = bf16[32,1024]{1,0:T(8,128)(2,1)S(1)} collective-permute-done((bf16[32,1024]{1,0:T(8,128)(2,1)S(1)}, bf16[32,1024]{1,0:T(8,128)(2,1)S(1)}, u32[]{:S(2)}, u32[]{:S(2)}) %collective-permute-start.1) | collective-permute-done | bytes 65568 | tf_op jit(solution)/shard_map/ppermute | solution.py:559
  11.2 1.4 %collective-permute-done.2.q3 = bf16[32,1024]{1,0:T(8,128)(2,1)S(1)} collective-permute-done((bf16[32,1024]{1,0:T(8,128)(2,1)S(1)}, bf16[32,1024]{1,0:T(8,128)(2,1)S(1)}, u32[]{:S(2)}, u32[]{:S(2)}) %collective-permute-start.2) | collective-permute-done | bytes 65568 | tf_op jit(solution)/shard_map/ppermute | solution.py:559
  12.6 1.2 %copy-done = bf16[64,2,64,512]{3,2,1,0:T(8,128)(2,1)S(1)} copy-done((bf16[64,2,64,512]{3,2,1,0:T(8,128)(2,1)S(1)}, bf16[64,2,64,512]{3,2,1,0:T(8,128)(2,1)}, u32[]{:S(2)}) %copy-start) | copy-done | bytes 8388632
  13.9 5.5 %attend.1 = (f32[32,1152]{1,0:T(8,128)S(1)}, bf16[32,1152]{1,0:T(8,128)(2,1)S(1)}, bf16[32,1152]{1,0:T(8,128)(2,1)S(1)}, bf16[32,1152]{1,0:T(8,128)(2,1)S(1)}, b...) custom-call(s32[8,128]{1,0:T(8,128)S(1)} %plan.1.meta_r, bf16[32,1024]{1,0:T(8,128)(2,1)S(1)} %gate.1.q0.q_ref, ...), custom_call_target="tpu_custom_call" | custom-call | flops 8589934592 | bytes 8388608 | tf_op jit(solution)/shard_map/attend/pallas_call | solution.py:647
  19.4 1.2 %collective-permute-start.3 = (bf16[32,1152]{1,0:T(8,128)(2,1)S(1)}, bf16[32,1152]{1,0:T(8,128)(2,1)S(1)}, u32[]{:S(2)}, u32[]{:S(2)}) collective-permute-start(bf16[32,1152]{1,0:T(8,128)(2,1)S(1)} %get-tuple-element.27), channel_id=1, source_target_pairs={{0,4},{4,0},{8,12},{12,8},{1,5},{5,1},{9,13},{13,9},{2,6},{6,2},{1... | collective-permute-start | bytes 221192 | tf_op jit(solution)/shard_map/ppermute | solution.py:559
  20.6 1.9 %collective-permute-start.4 = (bf16[32,1152]{1,0:T(8,128)(2,1)S(1)}, bf16[32,1152]{1,0:T(8,128)(2,1)S(1)}, u32[]{:S(2)}, u32[]{:S(2)}) collective-permute-start(bf16[32,1152]{1,0:T(8,128)(2,1)S(1)} %get-tuple-element.28), channel_id=1, source_target_pairs={{0,8},{4,12},{8,0},{12,4},{1,9},{5,13},{9,1},{13,5},{2,10},{6,14},... | collective-permute-start | bytes 221192 | tf_op jit(solution)/shard_map/ppermute | solution.py:559
  22.5 0.0 collective-permute-start.5
  22.5 3.3 %fresh.1 = (bf16[32,512]{1,0:T(8,128)(2,1)S(1)}, bf16[32,512]{1,0:T(8,128)(2,1)S(1)}, f32[32,1152]{1,0:T(8,128)S(1)}) custom-call(bf16[32,4608]{1,0:T(8,128)(2,1)S(1)} %get-tuple-element.23.n_ref, f32[32,256]{1,0:T(8,128)S(1)} %get-tuple-element.24.cs_ref, bf16[32,1024]{1,0:T(8,128)(2,1)S(1)} %gate.1.q0.q_ref, ...), custom_call_target="tpu_custom_call" | custom-call | flops 1825361152 | bytes 1782579 | tf_op jit(solution)/shard_map/fresh/pallas_call | solution.py:672
  25.9 0.8 %collective-permute-done.5.r3 = bf16[32,1152]{1,0:T(8,128)(2,1)S(1)} collective-permute-done((bf16[32,1152]{1,0:T(8,128)(2,1)S(1)}, bf16[32,1152]{1,0:T(8,128)(2,1)S(1)}, u32[]{:S(2)}, u32[]{:S(2)}) %collective-permute-start.5) | collective-permute-done | bytes 73760 | tf_op jit(solution)/shard_map/ppermute | solution.py:559
  26.7 1.9 %project.1 = (f32[32,1152]{1,0:T(8,128)S(1)}, bf16[32,1152]{1,0:T(8,128)(2,1)S(1)}, bf16[32,1152]{1,0:T(8,128)(2,1)S(1)}, bf16[32,1152]{1,0:T(8,128)(2,1)S(1)}) custom-call(bf16[1024,4608]{1,0:T(8,128)(2,1)S(1)} %get-tuple-element.21.w, f32[32,1152]{1,0:T(8,128)S(1)} %get-tuple-element.22.own, f32[32,1152]{1,0:T(8,128)S(1)} %get-tuple-element.26.sf, ...), custom_call_target="tpu_custom_call" | custom-call | flops 2040109440 | bytes 1992294 | tf_op jit(solution)/shard_map/project/pallas_call | solution.py:682
  28.6 2.0 %collective-permute-start.6 = (bf16[32,1152]{1,0:T(8,128)(2,1)S(1)}, bf16[32,1152]{1,0:T(8,128)(2,1)S(1)}, u32[]{:S(2)}, u32[]{:S(2)}) collective-permute-start(bf16[32,1152]{1,0:T(8,128)(2,1)S(1)} %get-tuple-element.31), channel_id=1, source_target_pairs={{0,1},{1,0},{2,3},{3,2},{4,5},{5,4},{6,7},{7,6},{8,9},{9,8},{10,11... | collective-permute-start | bytes 221192 | tf_op jit(solution)/shard_map/ppermute | solution.py:559
  30.6 2.6 %collective-permute-start.7 = (bf16[32,1152]{1,0:T(8,128)(2,1)S(1)}, bf16[32,1152]{1,0:T(8,128)(2,1)S(1)}, u32[]{:S(2)}, u32[]{:S(2)}) collective-permute-start(bf16[32,1152]{1,0:T(8,128)(2,1)S(1)} %get-tuple-element.32), channel_id=1, source_target_pairs={{0,2},{1,3},{2,0},{3,1},{4,6},{5,7},{6,4},{7,5},{8,10},{9,11},{10,... | collective-permute-start | bytes 221192 | tf_op jit(solution)/shard_map/ppermute | solution.py:559
  33.2 5.4 %collective-permute-done.7.r2 = bf16[32,1152]{1,0:T(8,128)(2,1)S(1)} collective-permute-done((bf16[32,1152]{1,0:T(8,128)(2,1)S(1)}, bf16[32,1152]{1,0:T(8,128)(2,1)S(1)}, u32[]{:S(2)}, u32[]{:S(2)}) %collective-permute-start.7) | collective-permute-done | bytes 73760 | tf_op jit(solution)/shard_map/ppermute | solution.py:559
  38.6 0.8 %collective-permute-done.8.r3 = bf16[32,1152]{1,0:T(8,128)(2,1)S(1)} collective-permute-done((bf16[32,1152]{1,0:T(8,128)(2,1)S(1)}, bf16[32,1152]{1,0:T(8,128)(2,1)S(1)}, u32[]{:S(2)}, u32[]{:S(2)}) %collective-permute-start.8) | collective-permute-done | bytes 73760 | tf_op jit(solution)/shard_map/ppermute | solution.py:559
  39.5 2.4 %collective-permute-start.10 = (f32[32,128]{1,0:T(8,128)S(1)}, f32[32,128]{1,0:T(8,128)S(1)}, u32[]{:S(2)}, u32[]{:S(2)}) collective-permute-start(f32[32,128]{1,0:T(8,128)S(1)} %get-tuple-element.35.s), channel_id=1, source_target_pairs={{0,2},{1,3},{2,0},{3,1},{4,6},{5,7},{6,4},{7,5},{8,10},{9,11},{10,... | collective-permute-start | bytes 49160 | tf_op jit(solution)/shard_map/ppermute | solution.py:559
  41.9 1.4 %collective-permute-start.11 = (f32[32,128]{1,0:T(8,128)S(1)}, f32[32,128]{1,0:T(8,128)S(1)}, u32[]{:S(2)}, u32[]{:S(2)}) collective-permute-start(f32[32,128]{1,0:T(8,128)S(1)} %get-tuple-element.35.s), channel_id=1, source_target_pairs={{0,3},{1,2},{2,1},{3,0},{4,7},{5,6},{6,5},{7,4},{8,11},{9,10},{10,... | collective-permute-start | bytes 49160 | tf_op jit(solution)/shard_map/ppermute | solution.py:559
  43.3 0.7 %copy.15 = bf16[32,2,512]{2,1,0:T(2,128)(2,1)} copy(bf16[32,2,512]{2,0,1:T(8,128)(2,1)S(1)} %pad_maximum_fusion) | data formatting | bytes 131072
  44.0 0.1 collective-permute-done.10.r2
  44.2 3.3 %collective-permute-done.11.r3 = f32[32,128]{1,0:T(8,128)S(1)} collective-permute-done((f32[32,128]{1,0:T(8,128)S(1)}, f32[32,128]{1,0:T(8,128)S(1)}, u32[]{:S(2)}, u32[]{:S(2)}) %collective-permute-start.11) | collective-permute-done | bytes 16416 | tf_op jit(solution)/shard_map/ppermute | solution.py:559
  47.4 0.7 %last.1 = bf16[32,1152]{1,0:T(8,128)(2,1)} custom-call(f32[32,1152]{1,0:T(8,128)S(1)} %get-tuple-element.34.t, f32[32,128]{1,0:T(8,128)S(1)} %get-tuple-element.35.s, f32[32,128]{1,0:T(8,128)S(1)} %collective-permute-done.9.r1, f32[32,128]{1,0:T(8,128)S(1)} %collective-permute-done.10.r2, f32[32,128]{1,0:T(8,128)S(1)} %collective-permute-done.11.r3, ...), custom_call_target="tpu_custom_call" | custom-call | flops 322122560 | bytes 314572 | tf_op jit(solution)/shard_map/last/pallas_call | solution.py:705
  (24 shorter events, 0.1 us)
Async XLA Ops:
  5.3 3.2 %copy-start.2 = (s32[128]{0:T(128)S(1)}, s32[128]{0:T(128)}, u32[]{:S(2)}) copy-start(s32[128]{0:T(128)} %lens_hbm.1) | copy-start | bytes 1540
  5.3 3.2 %copy-start.3 = (s32[128,32]{0,1:T(8,128)S(1)}, s32[128,32]{0,1:T(8,128)}, u32[]{:S(2)}) copy-start(s32[128,32]{0,1:T(8,128)} %param.23) | copy-start | bytes 49156
  5.4 3.2 %copy-start.4 = (s32[128]{0:T(128)S(1)}, s32[128]{0:T(128)}, u32[]{:S(2)}) copy-start(s32[128]{0:T(128)} %param.21) | copy-start | bytes 1540
  5.4 7.2 %slice-start = ((s8[16777216]{0:T(1024)(128)(4,1)}), s8[4194304]{0:T(1024)(128)(4,1)S(1)}, s32[]{:S(2)}) async-start(s8[16777216]{0:T(1024)(128)(4,1)} %bitcast.5), calls=%async_computation | async-start | bytes 8388608
  5.4 7.2 %slice-start.1 = ((s8[16777216]{0:T(1024)(128)(4,1)}), s8[4194304]{0:T(1024)(128)(4,1)S(1)}, s32[]{:S(2)}) async-start(s8[16777216]{0:T(1024)(128)(4,1)} %bitcast.5), calls=%async_computation.1 | async-start | bytes 8388608
  5.4 7.2 %slice-start.2 = ((s8[16777216]{0:T(1024)(128)(4,1)}), s8[4194304]{0:T(1024)(128)(4,1)S(1)}, s32[]{:S(2)}) async-start(s8[16777216]{0:T(1024)(128)(4,1)} %bitcast.5), calls=%async_computation.2 | async-start | bytes 8388608
  5.4 3.5 %collective-permute-start = (bf16[32,1024]{1,0:T(8,128)(2,1)S(1)}, bf16[32,1024]{1,0:T(8,128)(2,1)S(1)}, u32[]{:S(2)}, u32[]{:S(2)}) collective-permute-start(bf16[32,1024]{1,0:T(8,128)(2,1)S(1)} %gate.1.q0.q_ref), channel_id=1, source_target_pairs={{0,4},{4,0},{8,12},{12,8},{1,5},{5,1},{9,13},{13,9},{2,6},{6,2},{1... | collective-permute-start | bytes 196616 | tf_op jit(solution)/shard_map/ppermute | solution.py:559
  6.0 5.2 %collective-permute-start.1 = (bf16[32,1024]{1,0:T(8,128)(2,1)S(1)}, bf16[32,1024]{1,0:T(8,128)(2,1)S(1)}, u32[]{:S(2)}, u32[]{:S(2)}) collective-permute-start(bf16[32,1024]{1,0:T(8,128)(2,1)S(1)} %gate.1.q0.q_ref), channel_id=1, source_target_pairs={{0,8},{4,12},{8,0},{12,4},{1,9},{5,13},{9,1},{13,5},{2,10},{6,14},... | collective-permute-start | bytes 196616 | tf_op jit(solution)/shard_map/ppermute | solution.py:559
  8.5 4.1 %collective-permute-start.2 = (bf16[32,1024]{1,0:T(8,128)(2,1)S(1)}, bf16[32,1024]{1,0:T(8,128)(2,1)S(1)}, u32[]{:S(2)}, u32[]{:S(2)}) collective-permute-start(bf16[32,1024]{1,0:T(8,128)(2,1)S(1)} %gate.1.q0.q_ref), channel_id=1, source_target_pairs={{0,12},{4,8},{8,4},{12,0},{1,13},{5,9},{9,5},{13,1},{2,14},{6,10},... | collective-permute-start | bytes 196616 | tf_op jit(solution)/shard_map/ppermute | solution.py:559
  8.6 4.0 %slice-start.3 = ((s8[16777216]{0:T(1024)(128)(4,1)}), s8[4194304]{0:T(1024)(128)(4,1)S(1)}, s32[]{:S(2)}) async-start(s8[16777216]{0:T(1024)(128)(4,1)} %bitcast.5), calls=%async_computation.3 | async-start | bytes 8388608
  8.6 5.3 %copy-start = (bf16[64,2,64,512]{3,2,1,0:T(8,128)(2,1)S(1)}, bf16[64,2,64,512]{3,2,1,0:T(8,128)(2,1)}, u32[]{:S(2)}) copy-start(bf16[64,2,64,512]{3,2,1,0:T(8,128)(2,1)} %pr.1) | copy-start | bytes 25165828
  19.4 6.5 %collective-permute-start.3 = (bf16[32,1152]{1,0:T(8,128)(2,1)S(1)}, bf16[32,1152]{1,0:T(8,128)(2,1)S(1)}, u32[]{:S(2)}, u32[]{:S(2)}) collective-permute-start(bf16[32,1152]{1,0:T(8,128)(2,1)S(1)} %get-tuple-element.27), channel_id=1, source_target_pairs={{0,4},{4,0},{8,12},{12,8},{1,5},{5,1},{9,13},{13,9},{2,6},{6,2},{1... | collective-permute-start | bytes 221192 | tf_op jit(solution)/shard_map/ppermute | solution.py:559
  20.6 5.3 %collective-permute-start.4 = (bf16[32,1152]{1,0:T(8,128)(2,1)S(1)}, bf16[32,1152]{1,0:T(8,128)(2,1)S(1)}, u32[]{:S(2)}, u32[]{:S(2)}) collective-permute-start(bf16[32,1152]{1,0:T(8,128)(2,1)S(1)} %get-tuple-element.28), channel_id=1, source_target_pairs={{0,8},{4,12},{8,0},{12,4},{1,9},{5,13},{9,1},{13,5},{2,10},{6,14},... | collective-permute-start | bytes 221192 | tf_op jit(solution)/shard_map/ppermute | solution.py:559
  22.5 4.2 %collective-permute-start.5 = (bf16[32,1152]{1,0:T(8,128)(2,1)S(1)}, bf16[32,1152]{1,0:T(8,128)(2,1)S(1)}, u32[]{:S(2)}, u32[]{:S(2)}) collective-permute-start(bf16[32,1152]{1,0:T(8,128)(2,1)S(1)} %get-tuple-element.29), channel_id=1, source_target_pairs={{0,12},{4,8},{8,4},{12,0},{1,13},{5,9},{9,5},{13,1},{2,14},{6,10},... | collective-permute-start | bytes 221192 | tf_op jit(solution)/shard_map/ppermute | solution.py:559
  22.5 10.6 %copy-start.5 = (f32[1152]{0:T(1024)S(1)}, f32[1152]{0:T(1024)}, u32[]{:S(2)}) copy-start(f32[1152]{0:T(1024)} %param.18) | copy-start | bytes 13828
  22.5 24.9 %copy-start.1 = (bf16[32,4608]{1,0:T(8,128)(2,1)S(1)}, bf16[32,4608]{1,0:T(8,128)(2,1)}, u32[]{:S(2)}) copy-start(bf16[32,4608]{1,0:T(8,128)(2,1)} %hd.1) | copy-start | bytes 884740
  28.6 4.6 %collective-permute-start.6 = (bf16[32,1152]{1,0:T(8,128)(2,1)S(1)}, bf16[32,1152]{1,0:T(8,128)(2,1)S(1)}, u32[]{:S(2)}, u32[]{:S(2)}) collective-permute-start(bf16[32,1152]{1,0:T(8,128)(2,1)S(1)} %get-tuple-element.31), channel_id=1, source_target_pairs={{0,1},{1,0},{2,3},{3,2},{4,5},{5,4},{6,7},{7,6},{8,9},{9,8},{10,11... | collective-permute-start | bytes 221192 | tf_op jit(solution)/shard_map/ppermute | solution.py:559
  30.6 8.1 %collective-permute-start.7 = (bf16[32,1152]{1,0:T(8,128)(2,1)S(1)}, bf16[32,1152]{1,0:T(8,128)(2,1)S(1)}, u32[]{:S(2)}, u32[]{:S(2)}) collective-permute-start(bf16[32,1152]{1,0:T(8,128)(2,1)S(1)} %get-tuple-element.32), channel_id=1, source_target_pairs={{0,2},{1,3},{2,0},{3,1},{4,6},{5,7},{6,4},{7,5},{8,10},{9,11},{10,... | collective-permute-start | bytes 221192 | tf_op jit(solution)/shard_map/ppermute | solution.py:559
  33.2 6.3 %collective-permute-start.8 = (bf16[32,1152]{1,0:T(8,128)(2,1)S(1)}, bf16[32,1152]{1,0:T(8,128)(2,1)S(1)}, u32[]{:S(2)}, u32[]{:S(2)}) collective-permute-start(bf16[32,1152]{1,0:T(8,128)(2,1)S(1)} %get-tuple-element.33), channel_id=1, source_target_pairs={{0,3},{1,2},{2,1},{3,0},{4,7},{5,6},{6,5},{7,4},{8,11},{9,10},{10,... | collective-permute-start | bytes 221192 | tf_op jit(solution)/shard_map/ppermute | solution.py:559
  39.5 4.7 %collective-permute-start.10 = (f32[32,128]{1,0:T(8,128)S(1)}, f32[32,128]{1,0:T(8,128)S(1)}, u32[]{:S(2)}, u32[]{:S(2)}) collective-permute-start(f32[32,128]{1,0:T(8,128)S(1)} %get-tuple-element.35.s), channel_id=1, source_target_pairs={{0,2},{1,3},{2,0},{3,1},{4,6},{5,7},{6,4},{7,5},{8,10},{9,11},{10,... | collective-permute-start | bytes 49160 | tf_op jit(solution)/shard_map/ppermute | solution.py:559
  41.9 5.5 %collective-permute-start.11 = (f32[32,128]{1,0:T(8,128)S(1)}, f32[32,128]{1,0:T(8,128)S(1)}, u32[]{:S(2)}, u32[]{:S(2)}) collective-permute-start(f32[32,128]{1,0:T(8,128)S(1)} %get-tuple-element.35.s), channel_id=1, source_target_pairs={{0,3},{1,2},{2,1},{3,0},{4,7},{5,6},{6,5},{7,4},{8,11},{9,10},{10,... | collective-permute-start | bytes 49160 | tf_op jit(solution)/shard_map/ppermute | solution.py:559
  43.3 4.1 %collective-permute-start.9 = (f32[32,128]{1,0:T(8,128)S(1)}, f32[32,128]{1,0:T(8,128)S(1)}, u32[]{:S(2)}, u32[]{:S(2)}) collective-permute-start(f32[32,128]{1,0:T(8,128)S(1)} %get-tuple-element.35.s), channel_id=1, source_target_pairs={{0,1},{1,0},{2,3},{3,2},{4,5},{5,4},{6,7},{7,6},{8,9},{9,8},{10,11... | collective-permute-start | bytes 49160 | tf_op jit(solution)/shard_map/ppermute | solution.py:559

commit v3 on v2

--- a/solution.py
+++ b/solution.py
@@ -262,7 +262,7 @@
 
 
 CODE = 256
-AHEAD = 3
+AHEAD = 4
 
 
 def plan_kernel(pages, block_len, tasks, table_ref, lens_ref, task_ref, meta_ref):
@@ -308,8 +308,7 @@
 
 def attend_kernel(
     n_seq, score_scale, batch,
-    meta_hbm, q_refs, pages_ref, prompt_ref, far_refs, own_ref, msg_refs, near_refs,
-    meta_ref, qf, acc, acw, sem, far_sem,
+    meta_hbm, q_refs, pages_ref, prompt_ref, own_ref, near_ref, msg_ref, meta_ref, qf, acc, acw, sem,
 ):
     rows, width = q_refs[0].shape
     heads = width // LANES
@@ -320,10 +319,6 @@
     me = lax.axis_index("seq")
     fetch = pltpu.make_async_copy(meta_hbm, meta_ref, sem)
     fetch.start()
-    loads = []
-    for i, (far, near) in enumerate(zip(far_refs, near_refs)):
-        loads.append(pltpu.make_async_copy(far, near, far_sem.at[i]))
-        loads[-1].start()
     acc[...] = jnp.zeros_like(acc)
     acw[...] = jnp.zeros_like(acw)
     for k in range(n_seq):
@@ -390,7 +385,8 @@
                 add(owners[b][j], weights[b][j], collect(values[b][j * heads : (j + 1) * heads]))
         return c
 
-    lax.fori_loop(0, pages // (pair * batch), page_step, 0)
+    steps = pages // (pair * batch)
+    lax.fori_loop(0, steps, page_step, 0)
 
     count = meta_ref[2, 0]
     per = LANES // prompt_len
@@ -437,30 +433,39 @@
     for k in range(n_seq):
         base = (me ^ k) * (rows * heads)
         sums = jnp.zeros((rows, LANES), F32)
+        out = (own_ref, msg_ref.at[:rows], near_ref, msg_ref.at[rows:])[k]
         for h in range(heads):
             at = pl.ds(base + h, rows, stride=heads)
-            mix = acc[at, :]
+            out[:, h * LANES : (h + 1) * LANES] = acc[at, :].astype(out.dtype)
             tot = jnp.sum(acw[at, :], axis=1, keepdims=True)
-            if k == 0:
-                own_ref[:, h * LANES : (h + 1) * LANES] = mix
-                sums = jnp.where(lanes == h, tot, sums)
-            else:
-                msg_refs[k - 1][:, h * LANES : (h + 1) * LANES] = mix.astype(BF16)
-                top = tot.astype(BF16).astype(F32)
-                sums = jnp.where(lanes == h, top, jnp.where(lanes == heads + h, tot - top, sums))
-        if k == 0:
-            own_ref[:, heads * LANES :] = sums
-        else:
-            msg_refs[k - 1][:, heads * LANES :] = sums.astype(BF16)
-    for load in loads:
-        load.wait()
-
-
-def fresh_kernel(
-    score_scale, n_ref, cs_ref, q_ref, wk_ref, wv_hbm, k_ref, v_ref, self_ref, wv_ref, sem
-):
-    load = pltpu.make_async_copy(wv_hbm, wv_ref, sem)
-    load.start()
+            sums = jnp.where(lanes == h, tot, sums)
+        if k % 2:
+            sums = two_parts(sums, heads)
+        out[:, heads * LANES :] = sums.astype(out.dtype)
+
+
+def two_parts(sums, heads):
+    top = sums.astype(BF16).astype(F32)
+    return top + pltpu.roll(sums - top, heads, 1)
+
+
+def one_part(sums, heads):
+    whole = sums + pltpu.roll(sums, LANES - heads, 1)
+    return jnp.where(lane_iota(sums.shape[0]) < heads, whole, 0.0)
+
+
+def merge_kernel(near_ref, msg_ref, out_ref):
+    rows, wide = near_ref.shape
+    heads = wide // LANES - 1
+    for h in range(heads):
+        at = slice(h * LANES, (h + 1) * LANES)
+        out_ref[:, at] = (near_ref[:, at] + msg_ref[rows:, at].astype(F32)).astype(BF16)
+    at = slice(heads * LANES, wide)
+    sums = near_ref[:, at] + one_part(msg_ref[rows:, at].astype(F32), heads)
+    out_ref[:, at] = two_parts(sums, heads).astype(BF16)
+
+
+def fresh_kernel(score_scale, n_ref, cs_ref, q_ref, wk_ref, wv_ref, k_ref, v_ref, self_ref):
     rows, width = q_ref.shape
     heads = width // LANES
     kvh = k_ref.shape[1] // LANES
@@ -470,7 +475,6 @@
     cosine = cs_ref[:, :LANES]
     sines = cs_ref[:, LANES:]
     keys = jnp.dot(normed, wk_ref[...], preferred_element_type=F32)
-    load.wait()
     values = jnp.dot(normed, wv_ref[...], preferred_element_type=F32)
     lanes = lane_iota(rows)
     sums = jnp.zeros((rows, LANES), F32)
@@ -492,35 +496,31 @@
     self_ref[:, heads * LANES :] = sums
 
 
-def project_kernel(n_ten, w_ref, own_ref, self_ref, got_refs, p0_ref, out_refs):
-    _, wide = own_ref.shape
+def blend_kernel(n_ten, w_ref, own_ref, self_ref, msg_ref, got_ref, att_ref, *out_refs):
+    rows, wide = own_ref.shape
     heads = wide // LANES - 1
-    cols = p0_ref.shape[1]
-    at = slice(heads * LANES, (heads + 1) * LANES)
+    at = slice(heads * LANES, wide)
     sums = own_ref[:, at] + self_ref[:, at]
-    tail = None
-    for r in got_refs:
-        got = r[:, at].astype(F32)
-        tail = got if tail is None else tail + got
-    parts = []
+    sums = sums + one_part(msg_ref[:rows, at].astype(F32) + got_ref[:, at].astype(F32), heads)
     for h in range(heads):
         at = slice(h * LANES, (h + 1) * LANES)
         mix = own_ref[:, at] + self_ref[:, at]
-        for r in got_refs:
-            mix = mix + r[:, at].astype(F32)
-        tot = sums[:, h : h + 1]
-        if tail is not None:
-            tot = tot + tail[:, h : h + 1] + tail[:, heads + h : heads + h + 1]
-        parts.append((mix / tot).astype(BF16))
-    att = jnp.concatenate(parts, axis=1)
-    me = lax.axis_index("tensor")
-    for k in range(n_ten):
-        start = pl.multiple_of((me ^ k) * cols, LANES)
-        got = jnp.dot(att, w_ref[:, pl.ds(start, cols)], preferred_element_type=F32)
-        if k == 0:
-            p0_ref[...] = got
-        else:
-            out_refs[k - 1][...] = got.astype(BF16)
+        mix = mix + msg_ref[:rows, at].astype(F32) + got_ref[:, at].astype(F32)
+        att_ref[:, at] = (mix / sums[:, h : h + 1]).astype(BF16)
+    for i, out_ref in enumerate(out_refs):
+        project_part(n_ten - 1 - i, att_ref, w_ref, out_ref)
+
+
+def project_part(k, att_ref, w_ref, out_ref):
+    cols = out_ref.shape[1]
+    start = pl.multiple_of((lax.axis_index("tensor") ^ k) * cols, LANES)
+    got = jnp.dot(att_ref[...], w_ref[:, pl.ds(start, cols)], preferred_element_type=F32)
+    out_ref[...] = got.astype(out_ref.dtype)
+
+
+def project_kernel(w_ref, att_ref, *out_refs):
+    for k, out_ref in enumerate(out_refs):
+        project_part(k, att_ref, w_ref, out_ref)
 
 
 def sum_kernel(p0_ref, got_refs, sum_ref, sq_ref):
@@ -553,11 +553,8 @@
     return pltpu.CompilerParams(vmem_limit_bytes=mib << 20)
 
 
-def swap(arrays, axis, size):
-    got = []
-    for k, a in enumerate(arrays):
-        got.append(lax.ppermute(a, axis, [(i, i ^ (k + 1)) for i in range(size)]))
-    return got
+def swap(array, axis, size, k):
+    return lax.ppermute(array, axis, [(i, i ^ k) for i in range(size)])
 
 
 def split(depth, count):
@@ -633,65 +630,83 @@
         cost_estimate=cost(12),
         name="gate",
     )(query)
-    got = swap([query] * (n_seq - 1), "seq", n_seq)
+    near = swap(query, "seq", n_seq, 2)
+    side = swap(query, "seq", n_seq, 1)
+    far = swap(near, "seq", n_seq, 1)
     meta = pl.pallas_call(
         functools.partial(plan_kernel, pages, block_len, tasks),
         out_shape=shape((SUB, requests), jnp.int32),
         in_specs=[VM, VM, VM],
         out_specs=VM,
         compiler_params=params(1),
-        cost_estimate=cost(9),
+        cost_estimate=cost(0.3),
         name="plan",
     )(block_table.T, cache_lengths.reshape(1, requests), task_ids.reshape(1, requests))
-    batch = 32
-    outs = pl.pallas_call(
-        lambda meta_r, q0, q1, q2, q3, pg, pr, f1, f2, own, m1, m2, m3, n1, n2, *scratch: attend_kernel(
-            n_seq, score_scale, batch, meta_r, (q0, q1, q2, q3), pg, pr, (f1, f2),
-            own, (m1, m2, m3), (n1, n2), *scratch
+    batch = pages // 2
+    own, near, msg = pl.pallas_call(
+        lambda meta_r, q0, q1, q2, q3, *rest: attend_kernel(
+            n_seq, score_scale, batch, meta_r, (q0, q1, q2, q3), *rest
         ),
-        out_shape=(shape((rows, wide), F32),)
-        + (shape((rows, wide), BF16),) * (n_seq - 1)
-        + tuple(pltpu.VMEM(w.shape, w.dtype) for w in (w_key, w_out)),
-        in_specs=[HB] + [VM] * (n_seq + 2) + [HB] * 2,
-        out_specs=(VM,) * (n_seq + 2),
+        out_shape=(
+            shape((rows, wide), F32),
+            shape((rows, wide), F32),
+            shape((2 * rows, wide), BF16),
+        ),
+        in_specs=[HB] + [VM] * (n_seq + 2),
+        out_specs=(VM,) * 3,
         scratch_shapes=[
             pltpu.SMEM((SUB, requests), jnp.int32),
             pltpu.VMEM((requests * heads, LANES), F32),
             pltpu.VMEM((requests * heads, LANES), F32),
             pltpu.VMEM((requests * heads, LANES), F32),
             pltpu.SemaphoreType.DMA,
-            pltpu.SemaphoreType.DMA((2,)),
         ],
         compiler_params=params(A_MIB),
         cost_estimate=cost(8),
         name="attend",
-    )(meta, query, *got, cache_pool, prompt_cache, in_hbm(w_key), in_hbm(w_out))
-    own, msgs = outs[0], outs[1:n_seq]
-    key_near, out_near = outs[n_seq:]
-    got = swap(msgs, "seq", n_seq)
+    )(meta, query, side, near, far, cache_pool, prompt_cache)
+    msg = swap(msg, "seq", n_seq, 1)
+    merged = pl.pallas_call(
+        merge_kernel,
+        out_shape=shape((rows, wide), BF16),
+        in_specs=[VM] * 2,
+        out_specs=VM,
+        compiler_params=params(1),
+        cost_estimate=cost(0.1),
+        name="merge",
+    )(near, msg)
+    got = swap(merged, "seq", n_seq, 2)
     key_new, value_new, self_part = pl.pallas_call(
         functools.partial(fresh_kernel, score_scale),
         out_shape=(shape((rows, kv_width), BF16), shape((rows, kv_width), BF16), shape((rows, wide), F32)),
-        in_specs=[VM] * 4 + [HB],
+        in_specs=[VM] * 5,
         out_specs=(VM,) * 3,
-        scratch_shapes=[pltpu.VMEM(w_value.shape, BF16), pltpu.SemaphoreType.DMA],
         compiler_params=params(G_MIB),
         cost_estimate=cost(1.7),
         name="fresh",
-    )(normed, cs, query, key_near, in_hbm(w_value))
-    outs = pl.pallas_call(
-        lambda w, own, sf, r1, r2, r3, p0, o1, o2, o3: project_kernel(
-            n_ten, w, own, sf, (r1, r2, r3), p0, (o1, o2, o3)
-        ),
-        out_shape=(shape((rows, cols), F32),) + (shape((rows, cols), BF16),) * (n_ten - 1),
-        in_specs=[VM] * (3 + n_seq - 1),
-        out_specs=(VM,) * n_ten,
+    )(normed, cs, query, w_key, w_value)
+    att, part3, part2 = pl.pallas_call(
+        functools.partial(blend_kernel, n_ten),
+        out_shape=(shape((rows, width), BF16),) + (shape((rows, cols), BF16),) * 2,
+        in_specs=[VM] * 5,
+        out_specs=(VM,) * 3,
         compiler_params=params(H_MIB),
-        cost_estimate=cost(1.9),
+        cost_estimate=cost(0.7),
+        name="blend",
+    )(w_out, own, self_part, msg, got)
+    got3 = swap(part3, "tensor", n_ten, 3)
+    got2 = swap(part2, "tensor", n_ten, 2)
+    p0, part1 = pl.pallas_call(
+        project_kernel,
+        out_shape=(shape((rows, cols), F32), shape((rows, cols), BF16)),
+        in_specs=[VM] * 2,
+        out_specs=(VM,) * 2,
+        compiler_params=params(H_MIB),
+        cost_estimate=cost(1.3),
         name="project",
-    )(out_near, own, self_part, *got)
-    p0, parts = outs[0], outs[1:]
-    got = swap(parts, "tensor", n_ten)
+    )(w_out, att)
+    got1 = swap(part1, "tensor", n_ten, 1)
+    got = [got1, got2, got3]
     total, sq = pl.pallas_call(
         lambda p0, r1, r2, r3, t, s: sum_kernel(p0, (r1, r2, r3), t, s),
         out_shape=(shape((rows, cols), F32), shape((rows, LANES), F32)),
@@ -701,7 +716,7 @@
         cost_estimate=cost(0.3),
         name="sum",
     )(p0, *got)
-    got = swap([sq] * (n_ten - 1), "tensor", n_ten)
+    got = [swap(sq, "tensor", n_ten, k) for k in (1, 2, 3)]
     layer_out = pl.pallas_call(
         lambda t, s, r1, r2, r3, hd, g, o: last_kernel(t, s, (r1, r2, r3), hd, g, o),
         out_shape=shape((rows, cols), BF16),
@@ -715,9 +730,9 @@
     return (layer_out, fresh_cache)
 
 
-Q_MIB = 60
-A_MIB = 6
-G_MIB = 9
+Q_MIB = 52
+A_MIB = 4
+G_MIB = 4
 H_MIB = 4
 
 

time: 48.3 us -> 45.2 us (0.936)
  waiting for transfers between devices: 14.2 us -> 11.8 us
  Pallas kernels: 16.5 us -> 15.3 us
  starting transfers between devices: 14.7 us -> 15.8 us
  local copies, waits for them, and re-layouts: 2 us -> 1.27 us
    ppermute x12 -> x11, waiting for transfers between devices: 14.2 us -> 11.8 us  [swap(): return lax.ppermute(array, axis, [(i, i ^ k) for i in range(size)])]
    pallas_call x1, Pallas kernels: 3.33 us -> 1.73 us  [fast_body(): pl.pallas_call(functools.partial(fresh_kernel, score_scale), out_shape=(s...]
    ppermute x12 -> x11, starting transfers between devices: 14.7 us -> 15.8 us  [swap(): return lax.ppermute(array, axis, [(i, i ^ k) for i in range(size)])]
    unnamed x21 -> x31, local copies, waits for them, and re-layouts: 2 us -> 1.26 us
    pallas_call x2 -> x4, Pallas kernels: 7.37 us -> 7.73 us  [the longest x1 5.61 us: fast_body(): pl.pallas_call(lambda meta_r, q0, q1, q2, q3, *rest: attend_kernel(n_seq,...]
  transfers between devices with their start and end apart: 12 -> 11, of which waited for: 7 -> 9; matrix products, arithmetic and copies ran while one was open for 1% -> 2% of each run, Pallas kernels for 7% -> 6%
where the time goes in v3:
time: 45.2 us; the launch traced here: 45 us
  starting transfers between devices  15.8 us (35%)
  Pallas kernels  15.3 us (34%)
  waiting for transfers between devices  11.8 us (26%)
  local copies, waits for them, and re-layouts  1.27 us (3%)
  between operations  0.88 us (2%)
    ppermute x11, starting transfers between devices, swap(): return lax.ppermute(array, axis, [(i, i ^ k) for i in range(size)])  15.8 us
    ppermute x11, waiting for transfers between devices, swap(): return lax.ppermute(array, axis, [(i, i ^ k) for i in range(size)])  11.8 us
    pallas_call x1, Pallas kernels, fast_body(): pl.pallas_call(lambda meta_r, q0, q1, q2, q3, *rest: attend_kernel(n_seq,...  5.61 us
    pallas_call x1, Pallas kernels, fast_body(): pl.pallas_call(functools.partial(query_kernel, prompt_len, chunks), out_s...  4.76 us
    pallas_call x1, Pallas kernels, fast_body(): pl.pallas_call(functools.partial(fresh_kernel, score_scale), out_shape=(s...  1.73 us
    unnamed x31, local copies, waits for them, and re-layouts  1.26 us
    pallas_call x1, Pallas kernels, fast_body(): pl.pallas_call(functools.partial(blend_kernel, n_ten), out_shape=(shape((...  1.05 us
    pallas_call x1, Pallas kernels, fast_body(): pl.pallas_call(project_kernel, out_shape=(shape((rows, cols), F32), shape...  0.91 us
  transfers between devices with their start and end apart: 11, of which 9 were waited for; matrix products, arithmetic and copies ran while one was open for 2% of the time, Pallas kernels for 6%

profile of v3, /device:TPU:0, one launch (start us, length us, event | category | flops | bytes accessed | tf_op | source)
XLA Modules:
  0.0 45.0 jit_solution(11161615491434455240)
XLA Ops:
  0.6 4.8 %query.1 = (bf16[32,1024]{1,0:T(8,128)(2,1)S(1)}, bf16[32,4608]{1,0:T(8,128)(2,1)S(1)}, f32[32,256]{1,0:T(8,128)S(1)}) custom-call(s32[128]{0:T(128)} %lens_hbm.1, bf16[32,4608]{1,0:T(8,128)(2,1)} %hd.1, f32[4608]{0:T(1024)} %gain_hbm.1, bf16[4608,1024]{1,0:T(8,128)(2,1)} %w_ref.3), custom_call_target="tpu_custom_call" | custom-call | flops 53687092 | bytes 52428 | tf_op jit(solution)/shard_map/query/pallas_call | solution.py:602
  5.5 0.0 slice-start.8
  5.5 3.0 %collective-permute-start.1 = (bf16[32,1024]{1,0:T(8,128)(2,1)S(1)}, bf16[32,1024]{1,0:T(8,128)(2,1)S(1)}, u32[]{:S(2)}, u32[]{:S(2)}) collective-permute-start(bf16[32,1024]{1,0:T(8,128)(2,1)S(1)} %gate.1.q0.q_ref), channel_id=1, source_target_pairs={{0,8},{4,12},{8,0},{12,4},{1,9},{5,13},{9,1},{13,5},{2,10},{6,14},... | collective-permute-start | bytes 196616 | tf_op jit(solution)/shard_map/ppermute | solution.py:557
  8.5 2.2 %collective-permute-done.1.q2 = bf16[32,1024]{1,0:T(8,128)(2,1)S(1)} collective-permute-done((bf16[32,1024]{1,0:T(8,128)(2,1)S(1)}, bf16[32,1024]{1,0:T(8,128)(2,1)S(1)}, u32[]{:S(2)}, u32[]{:S(2)}) %collective-permute-start.1) | collective-permute-done | bytes 65568 | tf_op jit(solution)/shard_map/ppermute | solution.py:557
  10.8 0.0 slice-start.3
  10.8 0.3 plan.1.meta_r
  11.1 0.0 slice-start.4
  11.1 0.0 slice-start.6
  11.1 0.0 slice-start.1
  11.2 0.8 %collective-permute-done.2.q3 = bf16[32,1024]{1,0:T(8,128)(2,1)S(1)} collective-permute-done((bf16[32,1024]{1,0:T(8,128)(2,1)S(1)}, bf16[32,1024]{1,0:T(8,128)(2,1)S(1)}, u32[]{:S(2)}, u32[]{:S(2)}) %collective-permute-start.2) | collective-permute-done | bytes 65568 | tf_op jit(solution)/shard_map/ppermute | solution.py:557
  12.0 0.5 %slice-done.8 = s8[4194304]{0:T(1024)(128)(4,1)S(1)} async-done(((s8[8388608]{0:T(1024)(128)(4,1)}), s8[4194304]{0:T(1024)(128)(4,1)S(1)}, s32[]{:S(2)}) %slice-start.8) | async-done | bytes 4194328
  12.5 5.6 %attend.1 = (f32[32,1152]{1,0:T(8,128)S(1)}, f32[32,1152]{1,0:T(8,128)S(1)}, bf16[64,1152]{1,0:T(8,128)(2,1)S(1)}) custom-call(s32[8,128]{1,0:T(8,128)S(1)} %plan.1.meta_r, bf16[32,1024]{1,0:T(8,128)(2,1)S(1)} %gate.1.q0.q_ref, bf16[32,1024]{1,0:T(8,128)(2,1)S(1)} %collective-permute-done.q1, bf16[32,1024]{1,0:T(8,128)(2,1)S(1)} %collective-permute-done.1.q2, ...), custom_call_target="tpu_custom_call" | custom-call | flops 8589934592 | bytes 8388608 | tf_op jit(solution)/shard_map/attend/pallas_call | solution.py:646
  18.1 1.2 %collective-permute-start.3 = (bf16[64,1152]{1,0:T(8,128)(2,1)S(1)}, bf16[64,1152]{1,0:T(8,128)(2,1)S(1)}, u32[]{:S(2)}, u32[]{:S(2)}) collective-permute-start(bf16[64,1152]{1,0:T(8,128)(2,1)S(1)} %get-tuple-element.23), channel_id=1, source_target_pairs={{0,4},{4,0},{8,12},{12,8},{1,5},{5,1},{9,13},{13,9},{2,6},{6,2},{1... | collective-permute-start | bytes 442376 | tf_op jit(solution)/shard_map/ppermute | solution.py:557
  19.3 1.0 %collective-permute-done.3.msg_ref = bf16[64,1152]{1,0:T(8,128)(2,1)S(1)} collective-permute-done((bf16[64,1152]{1,0:T(8,128)(2,1)S(1)}, bf16[64,1152]{1,0:T(8,128)(2,1)S(1)}, u32[]{:S(2)}, u32[]{:S(2)}) %collective-permute-start.3) | collective-permute-done | bytes 147488 | tf_op jit(solution)/shard_map/ppermute | solution.py:557
  20.3 0.2 merge.1
  20.5 2.2 %collective-permute-start.4 = (bf16[32,1152]{1,0:T(8,128)(2,1)S(1)}, bf16[32,1152]{1,0:T(8,128)(2,1)S(1)}, u32[]{:S(2)}, u32[]{:S(2)}) collective-permute-start(bf16[32,1152]{1,0:T(8,128)(2,1)S(1)} %merge.1), channel_id=1, source_target_pairs={{0,8},{4,12},{8,0},{12,4},{1,9},{5,13},{9,1},{13,5},{2,10},{6,14},... | collective-permute-start | bytes 221192 | tf_op jit(solution)/shard_map/ppermute | solution.py:557
  22.7 1.7 %fresh.1 = (bf16[32,512]{1,0:T(8,128)(2,1)S(1)}, bf16[32,512]{1,0:T(8,128)(2,1)S(1)}, f32[32,1152]{1,0:T(8,128)S(1)}) custom-call(bf16[32,4608]{1,0:T(8,128)(2,1)S(1)} %get-tuple-element.20.n_ref, f32[32,256]{1,0:T(8,128)S(1)} %get-tuple-element.21.cs_ref, bf16[32,1024]{1,0:T(8,128)(2,1)S(1)} %gate.1.q0.q_ref, bf16[4608,512]{1,0:T(8,128)(2,1)S(1)} %bitcast.8, ...), custom_call_target="tpu_custom_call" | custom-call | flops 1825361152 | bytes 1782579 | tf_op jit(solution)/shard_map/fresh/pallas_call | solution.py:679
  24.5 0.8 %collective-permute-done.4.got_ref = bf16[32,1152]{1,0:T(8,128)(2,1)S(1)} collective-permute-done((bf16[32,1152]{1,0:T(8,128)(2,1)S(1)}, bf16[32,1152]{1,0:T(8,128)(2,1)S(1)}, u32[]{:S(2)}, u32[]{:S(2)}) %collective-permute-start.4) | collective-permute-done | bytes 73760 | tf_op jit(solution)/shard_map/ppermute | solution.py:557
  25.3 1.1 %blend.1 = (bf16[32,1024]{1,0:T(8,128)(2,1)S(1)}, bf16[32,1152]{1,0:T(8,128)(2,1)S(1)}, bf16[32,1152]{1,0:T(8,128)(2,1)S(1)}) custom-call(bf16[1024,4608]{1,0:T(8,128)(2,1)S(1)} %bitcast.6, f32[32,1152]{1,0:T(8,128)S(1)} %get-tuple-element.19.own_ref, f32[32,1152]{1,0:T(8,128)S(1)} %get-tuple-element.22.self_ref, ...), custom_call_target="tpu_custom_call" | custom-call | flops 751619264 | bytes 734003 | tf_op jit(solution)/shard_map/blend/pallas_call | solution.py:688
  26.4 3.2 %collective-permute-start.6 = (bf16[32,1152]{1,0:T(8,128)(2,1)S(1)}, bf16[32,1152]{1,0:T(8,128)(2,1)S(1)}, u32[]{:S(2)}, u32[]{:S(2)}) collective-permute-start(bf16[32,1152]{1,0:T(8,128)(2,1)S(1)} %get-tuple-element.28), channel_id=1, source_target_pairs={{0,2},{1,3},{2,0},{3,1},{4,6},{5,7},{6,4},{7,5},{8,10},{9,11},{10,... | collective-permute-start | bytes 221192 | tf_op jit(solution)/shard_map/ppermute | solution.py:557
  29.6 1.4 %collective-permute-start.7 = (bf16[32,1152]{1,0:T(8,128)(2,1)S(1)}, bf16[32,1152]{1,0:T(8,128)(2,1)S(1)}, u32[]{:S(2)}, u32[]{:S(2)}) collective-permute-start(bf16[32,1152]{1,0:T(8,128)(2,1)S(1)} %get-tuple-element.29), channel_id=1, source_target_pairs={{0,3},{1,2},{2,1},{3,0},{4,7},{5,6},{6,5},{7,4},{8,11},{9,10},{10,... | collective-permute-start | bytes 221192 | tf_op jit(solution)/shard_map/ppermute | solution.py:557
  30.9 0.9 %project.1 = (f32[32,1152]{1,0:T(8,128)S(1)}, bf16[32,1152]{1,0:T(8,128)(2,1)S(1)}) custom-call(bf16[1024,4608]{1,0:T(8,128)(2,1)S(1)} %bitcast.6, bf16[32,1024]{1,0:T(8,128)(2,1)S(1)} %get-tuple-element.25.att_ref), custom_call_target="tpu_custom_call" | custom-call | flops 1395864320 | bytes 1363148 | tf_op jit(solution)/shard_map/project/pallas_call | solution.py:699
  31.9 0.3 collective-permute-start.5
  32.2 2.2 %collective-permute-done.6.r2 = bf16[32,1152]{1,0:T(8,128)(2,1)S(1)} collective-permute-done((bf16[32,1152]{1,0:T(8,128)(2,1)S(1)}, bf16[32,1152]{1,0:T(8,128)(2,1)S(1)}, u32[]{:S(2)}, u32[]{:S(2)}) %collective-permute-start.6) | collective-permute-done | bytes 73760 | tf_op jit(solution)/shard_map/ppermute | solution.py:557
  34.4 1.9 %collective-permute-done.7.r3 = bf16[32,1152]{1,0:T(8,128)(2,1)S(1)} collective-permute-done((bf16[32,1152]{1,0:T(8,128)(2,1)S(1)}, bf16[32,1152]{1,0:T(8,128)(2,1)S(1)}, u32[]{:S(2)}, u32[]{:S(2)}) %collective-permute-start.7) | collective-permute-done | bytes 73760 | tf_op jit(solution)/shard_map/ppermute | solution.py:557
  36.3 0.5 %collective-permute-done.5.r1 = bf16[32,1152]{1,0:T(8,128)(2,1)S(1)} collective-permute-done((bf16[32,1152]{1,0:T(8,128)(2,1)S(1)}, bf16[32,1152]{1,0:T(8,128)(2,1)S(1)}, u32[]{:S(2)}, u32[]{:S(2)}) %collective-permute-start.5) | collective-permute-done | bytes 73760 | tf_op jit(solution)/shard_map/ppermute | solution.py:557
  36.9 2.8 %collective-permute-start.10 = (f32[32,128]{1,0:T(8,128)S(1)}, f32[32,128]{1,0:T(8,128)S(1)}, u32[]{:S(2)}, u32[]{:S(2)}) collective-permute-start(f32[32,128]{1,0:T(8,128)S(1)} %get-tuple-element.31.s), channel_id=1, source_target_pairs={{0,3},{1,2},{2,1},{3,0},{4,7},{5,6},{6,5},{7,4},{8,11},{9,10},{10,... | collective-permute-start | bytes 49160 | tf_op jit(solution)/shard_map/ppermute | solution.py:557
  39.6 1.7 %collective-permute-start.8 = (f32[32,128]{1,0:T(8,128)S(1)}, f32[32,128]{1,0:T(8,128)S(1)}, u32[]{:S(2)}, u32[]{:S(2)}) collective-permute-start(f32[32,128]{1,0:T(8,128)S(1)} %get-tuple-element.31.s), channel_id=1, source_target_pairs={{0,1},{1,0},{2,3},{3,2},{4,5},{5,4},{6,7},{7,6},{8,9},{9,8},{10,11... | collective-permute-start | bytes 49160 | tf_op jit(solution)/shard_map/ppermute | solution.py:557
  41.3 0.7 %copy.15 = bf16[32,2,512]{2,1,0:T(2,128)(2,1)} copy(bf16[32,2,512]{2,0,1:T(8,128)(2,1)S(1)} %pad_maximum_fusion) | data formatting | bytes 131072
  42.0 0.4 collective-permute-done.10.r3
  42.5 1.8 %collective-permute-done.9.r2 = f32[32,128]{1,0:T(8,128)S(1)} collective-permute-done((f32[32,128]{1,0:T(8,128)S(1)}, f32[32,128]{1,0:T(8,128)S(1)}, u32[]{:S(2)}, u32[]{:S(2)}) %collective-permute-start.9) | collective-permute-done | bytes 16416 | tf_op jit(solution)/shard_map/ppermute | solution.py:557
  44.3 0.7 %last.1 = bf16[32,1152]{1,0:T(8,128)(2,1)} custom-call(f32[32,1152]{1,0:T(8,128)S(1)} %get-tuple-element.30.t, f32[32,128]{1,0:T(8,128)S(1)} %get-tuple-element.31.s, f32[32,128]{1,0:T(8,128)S(1)} %collective-permute-done.8.r1, f32[32,128]{1,0:T(8,128)S(1)} %collective-permute-done.9.r2, f32[32,128]{1,0:T(8,128)S(1)} %collective-permute-done.10.r3, ...), custom_call_target="tpu_custom_call" | custom-call | flops 322122560 | bytes 314572 | tf_op jit(solution)/shard_map/last/pallas_call | solution.py:720
  (37 shorter events, 0.2 us)
Async XLA Ops:
  0.6 11.4 %slice-start.7 = ((s8[8388608]{0:T(1024)(128)(4,1)}), s8[4194304]{0:T(1024)(128)(4,1)S(1)}, s32[]{:S(2)}) async-start(s8[8388608]{0:T(1024)(128)(4,1)} %bitcast.14), calls=%async_computation.7 | async-start | bytes 8388608
  5.4 5.4 %copy-start.1 = (s32[128]{0:T(128)S(1)}, s32[128]{0:T(128)}, u32[]{:S(2)}) copy-start(s32[128]{0:T(128)} %lens_hbm.1) | copy-start | bytes 1540
  5.4 5.3 %copy-start.3 = (s32[128,32]{0,1:T(8,128)S(1)}, s32[128,32]{0,1:T(8,128)}, u32[]{:S(2)}) copy-start(s32[128,32]{0,1:T(8,128)} %param.23) | copy-start | bytes 49156
  5.4 5.3 %copy-start.4 = (s32[128]{0:T(128)S(1)}, s32[128]{0:T(128)}, u32[]{:S(2)}) copy-start(s32[128]{0:T(128)} %param.21) | copy-start | bytes 1540
  5.4 6.6 %copy-start.2 = (bf16[64,2,128,512]{3,2,1,0:T(8,128)(2,1)S(1)}, bf16[64,2,128,512]{3,2,1,0:T(8,128)(2,1)}, u32[]{:S(2)}) copy-start(bf16[64,2,128,512]{3,2,1,0:T(8,128)(2,1)} %rest_0_.1) | copy-start | bytes 50331652
  5.5 7.0 %slice-start.8 = ((s8[8388608]{0:T(1024)(128)(4,1)}), s8[4194304]{0:T(1024)(128)(4,1)S(1)}, s32[]{:S(2)}) async-start(s8[8388608]{0:T(1024)(128)(4,1)} %bitcast.14), calls=%async_computation.8 | async-start | bytes 8388608
  5.5 5.3 %collective-permute-start.1 = (bf16[32,1024]{1,0:T(8,128)(2,1)S(1)}, bf16[32,1024]{1,0:T(8,128)(2,1)S(1)}, u32[]{:S(2)}, u32[]{:S(2)}) collective-permute-start(bf16[32,1024]{1,0:T(8,128)(2,1)S(1)} %gate.1.q0.q_ref), channel_id=1, source_target_pairs={{0,8},{4,12},{8,0},{12,4},{1,9},{5,13},{9,1},{13,5},{2,10},{6,14},... | collective-permute-start | bytes 196616 | tf_op jit(solution)/shard_map/ppermute | solution.py:557
  8.5 2.6 %collective-permute-start = (bf16[32,1024]{1,0:T(8,128)(2,1)S(1)}, bf16[32,1024]{1,0:T(8,128)(2,1)S(1)}, u32[]{:S(2)}, u32[]{:S(2)}) collective-permute-start(bf16[32,1024]{1,0:T(8,128)(2,1)S(1)} %gate.1.q0.q_ref), channel_id=1, source_target_pairs={{0,4},{4,0},{8,12},{12,8},{1,5},{5,1},{9,13},{13,9},{2,6},{6,2},{1... | collective-permute-start | bytes 196616 | tf_op jit(solution)/shard_map/ppermute | solution.py:557
  10.8 1.3 %collective-permute-start.2 = (bf16[32,1024]{1,0:T(8,128)(2,1)S(1)}, bf16[32,1024]{1,0:T(8,128)(2,1)S(1)}, u32[]{:S(2)}, u32[]{:S(2)}) collective-permute-start(bf16[32,1024]{1,0:T(8,128)(2,1)S(1)} %collective-permute-done.1.q2), channel_id=1, source_target_pairs={{0,4},{4,0},{8,12},{12,8},{1,5},{5,1},{9,13},{13,9},{2,6},{6,2},{1... | collective-permute-start | bytes 196616 | tf_op jit(solution)/shard_map/ppermute | solution.py:557
  10.8 11.9 %slice-start.3 = ((s8[4718592]{0:T(1024)(128)(4,1)}), s8[4194304]{0:T(1024)(128)(4,1)S(1)}, s32[]{:S(2)}) async-start(s8[4718592]{0:T(1024)(128)(4,1)} %bitcast.7), calls=%async_computation.3 | async-start | bytes 8388608
  10.8 11.9 %slice-start.5 = ((s8[4718592]{0:T(1024)(128)(4,1)}), s8[4194304]{0:T(1024)(128)(4,1)S(1)}, s32[]{:S(2)}) async-start(s8[4718592]{0:T(1024)(128)(4,1)} %bitcast.9), calls=%async_computation.5 | async-start | bytes 8388608
  10.8 14.5 %slice-start = ((s8[9437184]{0:T(1024)(128)(4,1)}), s8[4194304]{0:T(1024)(128)(4,1)S(1)}, s32[]{:S(2)}) async-start(s8[9437184]{0:T(1024)(128)(4,1)} %bitcast.5), calls=%async_computation | async-start | bytes 8388608
  11.1 11.6 %slice-start.4 = ((s8[4718592]{0:T(1024)(128)(4,1)}), s8[524288]{0:T(1024)(128)(4,1)S(1)}, s32[]{:S(2)}) async-start(s8[4718592]{0:T(1024)(128)(4,1)} %bitcast.7), calls=%async_computation.4 | async-start | bytes 1048576
  11.1 11.6 %slice-start.6 = ((s8[4718592]{0:T(1024)(128)(4,1)}), s8[524288]{0:T(1024)(128)(4,1)S(1)}, s32[]{:S(2)}) async-start(s8[4718592]{0:T(1024)(128)(4,1)} %bitcast.9), calls=%async_computation.6 | async-start | bytes 1048576
  11.1 14.1 %slice-start.1 = ((s8[9437184]{0:T(1024)(128)(4,1)}), s8[4194304]{0:T(1024)(128)(4,1)S(1)}, s32[]{:S(2)}) async-start(s8[9437184]{0:T(1024)(128)(4,1)} %bitcast.5), calls=%async_computation.1 | async-start | bytes 8388608
  11.1 14.1 %slice-start.2 = ((s8[9437184]{0:T(1024)(128)(4,1)}), s8[1048576]{0:T(1024)(128)(4,1)S(1)}, s32[]{:S(2)}) async-start(s8[9437184]{0:T(1024)(128)(4,1)} %bitcast.5), calls=%async_computation.2 | async-start | bytes 2097152
  18.1 2.2 %collective-permute-start.3 = (bf16[64,1152]{1,0:T(8,128)(2,1)S(1)}, bf16[64,1152]{1,0:T(8,128)(2,1)S(1)}, u32[]{:S(2)}, u32[]{:S(2)}) collective-permute-start(bf16[64,1152]{1,0:T(8,128)(2,1)S(1)} %get-tuple-element.23), channel_id=1, source_target_pairs={{0,4},{4,0},{8,12},{12,8},{1,5},{5,1},{9,13},{13,9},{2,6},{6,2},{1... | collective-permute-start | bytes 442376 | tf_op jit(solution)/shard_map/ppermute | solution.py:557
  20.5 4.8 %collective-permute-start.4 = (bf16[32,1152]{1,0:T(8,128)(2,1)S(1)}, bf16[32,1152]{1,0:T(8,128)(2,1)S(1)}, u32[]{:S(2)}, u32[]{:S(2)}) collective-permute-start(bf16[32,1152]{1,0:T(8,128)(2,1)S(1)} %merge.1), channel_id=1, source_target_pairs={{0,8},{4,12},{8,0},{12,4},{1,9},{5,13},{9,1},{13,5},{2,10},{6,14},... | collective-permute-start | bytes 221192 | tf_op jit(solution)/shard_map/ppermute | solution.py:557
  25.3 16.0 %copy-start.5 = (f32[1152]{0:T(1024)S(1)}, f32[1152]{0:T(1024)}, u32[]{:S(2)}) copy-start(f32[1152]{0:T(1024)} %param.18) | copy-start | bytes 13828
  25.3 19.0 %copy-start = (bf16[32,4608]{1,0:T(8,128)(2,1)S(1)}, bf16[32,4608]{1,0:T(8,128)(2,1)}, u32[]{:S(2)}) copy-start(bf16[32,4608]{1,0:T(8,128)(2,1)} %hd.1) | copy-start | bytes 884740
  26.4 8.0 %collective-permute-start.6 = (bf16[32,1152]{1,0:T(8,128)(2,1)S(1)}, bf16[32,1152]{1,0:T(8,128)(2,1)S(1)}, u32[]{:S(2)}, u32[]{:S(2)}) collective-permute-start(bf16[32,1152]{1,0:T(8,128)(2,1)S(1)} %get-tuple-element.28), channel_id=1, source_target_pairs={{0,2},{1,3},{2,0},{3,1},{4,6},{5,7},{6,4},{7,5},{8,10},{9,11},{10,... | collective-permute-start | bytes 221192 | tf_op jit(solution)/shard_map/ppermute | solution.py:557
  29.6 6.7 %collective-permute-start.7 = (bf16[32,1152]{1,0:T(8,128)(2,1)S(1)}, bf16[32,1152]{1,0:T(8,128)(2,1)S(1)}, u32[]{:S(2)}, u32[]{:S(2)}) collective-permute-start(bf16[32,1152]{1,0:T(8,128)(2,1)S(1)} %get-tuple-element.29), channel_id=1, source_target_pairs={{0,3},{1,2},{2,1},{3,0},{4,7},{5,6},{6,5},{7,4},{8,11},{9,10},{10,... | collective-permute-start | bytes 221192 | tf_op jit(solution)/shard_map/ppermute | solution.py:557
  31.9 4.9 %collective-permute-start.5 = (bf16[32,1152]{1,0:T(8,128)(2,1)S(1)}, bf16[32,1152]{1,0:T(8,128)(2,1)S(1)}, u32[]{:S(2)}, u32[]{:S(2)}) collective-permute-start(bf16[32,1152]{1,0:T(8,128)(2,1)S(1)} %get-tuple-element.27), channel_id=1, source_target_pairs={{0,1},{1,0},{2,3},{3,2},{4,5},{5,4},{6,7},{7,6},{8,9},{9,8},{10,11... | collective-permute-start | bytes 221192 | tf_op jit(solution)/shard_map/ppermute | solution.py:557
  36.9 5.6 %collective-permute-start.10 = (f32[32,128]{1,0:T(8,128)S(1)}, f32[32,128]{1,0:T(8,128)S(1)}, u32[]{:S(2)}, u32[]{:S(2)}) collective-permute-start(f32[32,128]{1,0:T(8,128)S(1)} %get-tuple-element.31.s), channel_id=1, source_target_pairs={{0,3},{1,2},{2,1},{3,0},{4,7},{5,6},{6,5},{7,4},{8,11},{9,10},{10,... | collective-permute-start | bytes 49160 | tf_op jit(solution)/shard_map/ppermute | solution.py:557
  39.6 4.6 %collective-permute-start.9 = (f32[32,128]{1,0:T(8,128)S(1)}, f32[32,128]{1,0:T(8,128)S(1)}, u32[]{:S(2)}, u32[]{:S(2)}) collective-permute-start(f32[32,128]{1,0:T(8,128)S(1)} %get-tuple-element.31.s), channel_id=1, source_target_pairs={{0,2},{1,3},{2,0},{3,1},{4,6},{5,7},{6,4},{7,5},{8,10},{9,11},{10,... | collective-permute-start | bytes 49160 | tf_op jit(solution)/shard_map/ppermute | solution.py:557
  39.6 4.6 %collective-permute-start.8 = (f32[32,128]{1,0:T(8,128)S(1)}, f32[32,128]{1,0:T(8,128)S(1)}, u32[]{:S(2)}, u32[]{:S(2)}) collective-permute-start(f32[32,128]{1,0:T(8,128)S(1)} %get-tuple-element.31.s), channel_id=1, source_target_pairs={{0,1},{1,0},{2,3},{3,2},{4,5},{5,4},{6,7},{7,6},{8,9},{9,8},{10,11... | collective-permute-start | bytes 49160 | tf_op jit(solution)/shard_map/ppermute | solution.py:557

commit v4 on v3

--- a/solution.py
+++ b/solution.py
@@ -617,7 +617,7 @@
             pltpu.SemaphoreType.DMA((3,)),
         ],
         compiler_params=params(Q_MIB),
-        cost_estimate=cost(0.05),
+        cost_estimate=cost(4),
         name="query",
     )(*[in_hbm(a) for a in (cache_lengths, hidden, pre_gain, w_query)])
     query = pl.pallas_call(
@@ -627,7 +627,7 @@
         out_specs=VM,
         input_output_aliases={0: 0},
         compiler_params=params(1),
-        cost_estimate=cost(12),
+        cost_estimate=cost(5),
         name="gate",
     )(query)
     near = swap(query, "seq", n_seq, 2)
@@ -730,7 +730,7 @@
     return (layer_out, fresh_cache)
 
 
-Q_MIB = 52
+Q_MIB = 48
 A_MIB = 4
 G_MIB = 4
 H_MIB = 4

time: 45.2 us -> 44.7 us (0.989)
  local copies, waits for them, and re-layouts: 1.27 us -> 0.8 us
    unnamed x31 -> x29, local copies, waits for them, and re-layouts: 1.26 us -> 0.79 us
  transfers between devices with their start and end apart: 11 -> 11, of which waited for: 9 -> 9; matrix products, arithmetic and copies ran while one was open for 2% -> 2% of each run, Pallas kernels for 6% -> 7%
where the time goes in v4:
time: 44.7 us; the launch traced here: 44.5 us
  starting transfers between devices  15.8 us (35%)
  Pallas kernels  15.3 us (34%)
  waiting for transfers between devices  11.8 us (26%)
  between operations  0.87 us (2%)
  local copies, waits for them, and re-layouts  0.8 us (2%)
    ppermute x11, starting transfers between devices, swap(): return lax.ppermute(array, axis, [(i, i ^ k) for i in range(size)])  15.8 us
    ppermute x11, waiting for transfers between devices, swap(): return lax.ppermute(array, axis, [(i, i ^ k) for i in range(size)])  11.8 us
    pallas_call x1, Pallas kernels, fast_body(): pl.pallas_call(lambda meta_r, q0, q1, q2, q3, *rest: attend_kernel(n_seq,...  5.61 us
    pallas_call x1, Pallas kernels, fast_body(): pl.pallas_call(functools.partial(query_kernel, prompt_len, chunks), out_s...  4.76 us
    pallas_call x1, Pallas kernels, fast_body(): pl.pallas_call(functools.partial(fresh_kernel, score_scale), out_shape=(s...  1.73 us
    pallas_call x1, Pallas kernels, fast_body(): pl.pallas_call(functools.partial(blend_kernel, n_ten), out_shape=(shape((...  1.06 us
    pallas_call x1, Pallas kernels, fast_body(): pl.pallas_call(project_kernel, out_shape=(shape((rows, cols), F32), shape...  0.91 us
  transfers between devices with their start and end apart: 11, of which 9 were waited for; matrix products, arithmetic and copies ran while one was open for 2% of the time, Pallas kernels for 7%

profile of v4, /device:TPU:0, one launch (start us, length us, event | category | flops | bytes accessed | tf_op | source)
XLA Modules:
  0.0 44.5 jit_solution(10286443987099286308)
XLA Ops:
  0.6 4.8 %query.1 = (bf16[32,1024]{1,0:T(8,128)(2,1)S(1)}, bf16[32,4608]{1,0:T(8,128)(2,1)S(1)}, f32[32,256]{1,0:T(8,128)S(1)}) custom-call(s32[128]{0:T(128)} %lens_hbm.1, bf16[32,4608]{1,0:T(8,128)(2,1)} %hd.1, f32[4608]{0:T(1024)} %gain_hbm.1, bf16[4608,1024]{1,0:T(8,128)(2,1)} %w_ref.3), custom_call_target="tpu_custom_call" | custom-call | flops 4294967296 | bytes 4194304 | tf_op jit(solution)/shard_map/query/pallas_call | solution.py:602
  5.5 3.0 %collective-permute-start.1 = (bf16[32,1024]{1,0:T(8,128)(2,1)S(1)}, bf16[32,1024]{1,0:T(8,128)(2,1)S(1)}, u32[]{:S(2)}, u32[]{:S(2)}) collective-permute-start(bf16[32,1024]{1,0:T(8,128)(2,1)S(1)} %gate.1.q0.q_ref), channel_id=1, source_target_pairs={{0,8},{4,12},{8,0},{12,4},{1,9},{5,13},{9,1},{13,5},{2,10},{6,14},... | collective-permute-start | bytes 196616 | tf_op jit(solution)/shard_map/ppermute | solution.py:557
  8.5 2.2 %collective-permute-done.1.q2 = bf16[32,1024]{1,0:T(8,128)(2,1)S(1)} collective-permute-done((bf16[32,1024]{1,0:T(8,128)(2,1)S(1)}, bf16[32,1024]{1,0:T(8,128)(2,1)S(1)}, u32[]{:S(2)}, u32[]{:S(2)}) %collective-permute-start.1) | collective-permute-done | bytes 65568 | tf_op jit(solution)/shard_map/ppermute | solution.py:557
  10.8 0.0 slice-start.3
  10.8 0.0 slice-start.5
  10.8 0.0 slice-start
  10.8 0.3 plan.1.meta_r
  11.1 0.0 slice-start.4
  11.1 0.0 slice-start.6
  11.1 0.0 slice-start.1
  11.2 0.8 %collective-permute-done.2.q3 = bf16[32,1024]{1,0:T(8,128)(2,1)S(1)} collective-permute-done((bf16[32,1024]{1,0:T(8,128)(2,1)S(1)}, bf16[32,1024]{1,0:T(8,128)(2,1)S(1)}, u32[]{:S(2)}, u32[]{:S(2)}) %collective-permute-start.2) | collective-permute-done | bytes 65568 | tf_op jit(solution)/shard_map/ppermute | solution.py:557
  12.0 5.6 %attend.1 = (f32[32,1152]{1,0:T(8,128)S(1)}, f32[32,1152]{1,0:T(8,128)S(1)}, bf16[64,1152]{1,0:T(8,128)(2,1)S(1)}) custom-call(s32[8,128]{1,0:T(8,128)S(1)} %plan.1.meta_r, bf16[32,1024]{1,0:T(8,128)(2,1)S(1)} %gate.1.q0.q_ref, bf16[32,1024]{1,0:T(8,128)(2,1)S(1)} %collective-permute-done.q1, bf16[32,1024]{1,0:T(8,128)(2,1)S(1)} %collective-permute-done.1.q2, ...), custom_call_target="tpu_custom_call" | custom-call | flops 8589934592 | bytes 8388608 | tf_op jit(solution)/shard_map/attend/pallas_call | solution.py:646
  17.6 1.2 %collective-permute-start.3 = (bf16[64,1152]{1,0:T(8,128)(2,1)S(1)}, bf16[64,1152]{1,0:T(8,128)(2,1)S(1)}, u32[]{:S(2)}, u32[]{:S(2)}) collective-permute-start(bf16[64,1152]{1,0:T(8,128)(2,1)S(1)} %get-tuple-element.23), channel_id=1, source_target_pairs={{0,4},{4,0},{8,12},{12,8},{1,5},{5,1},{9,13},{13,9},{2,6},{6,2},{1... | collective-permute-start | bytes 442376 | tf_op jit(solution)/shard_map/ppermute | solution.py:557
  18.8 1.0 %collective-permute-done.3.msg_ref = bf16[64,1152]{1,0:T(8,128)(2,1)S(1)} collective-permute-done((bf16[64,1152]{1,0:T(8,128)(2,1)S(1)}, bf16[64,1152]{1,0:T(8,128)(2,1)S(1)}, u32[]{:S(2)}, u32[]{:S(2)}) %collective-permute-start.3) | collective-permute-done | bytes 147488 | tf_op jit(solution)/shard_map/ppermute | solution.py:557
  19.8 0.2 merge.1
  20.0 2.2 %collective-permute-start.4 = (bf16[32,1152]{1,0:T(8,128)(2,1)S(1)}, bf16[32,1152]{1,0:T(8,128)(2,1)S(1)}, u32[]{:S(2)}, u32[]{:S(2)}) collective-permute-start(bf16[32,1152]{1,0:T(8,128)(2,1)S(1)} %merge.1), channel_id=1, source_target_pairs={{0,8},{4,12},{8,0},{12,4},{1,9},{5,13},{9,1},{13,5},{2,10},{6,14},... | collective-permute-start | bytes 221192 | tf_op jit(solution)/shard_map/ppermute | solution.py:557
  22.2 1.7 %fresh.1 = (bf16[32,512]{1,0:T(8,128)(2,1)S(1)}, bf16[32,512]{1,0:T(8,128)(2,1)S(1)}, f32[32,1152]{1,0:T(8,128)S(1)}) custom-call(bf16[32,4608]{1,0:T(8,128)(2,1)S(1)} %get-tuple-element.20.n_ref, f32[32,256]{1,0:T(8,128)S(1)} %get-tuple-element.21.cs_ref, bf16[32,1024]{1,0:T(8,128)(2,1)S(1)} %gate.1.q0.q_ref, bf16[4608,512]{1,0:T(8,128)(2,1)S(1)} %bitcast.8, ...), custom_call_target="tpu_custom_call" | custom-call | flops 1825361152 | bytes 1782579 | tf_op jit(solution)/shard_map/fresh/pallas_call | solution.py:679
  24.0 0.8 %collective-permute-done.4.got_ref = bf16[32,1152]{1,0:T(8,128)(2,1)S(1)} collective-permute-done((bf16[32,1152]{1,0:T(8,128)(2,1)S(1)}, bf16[32,1152]{1,0:T(8,128)(2,1)S(1)}, u32[]{:S(2)}, u32[]{:S(2)}) %collective-permute-start.4) | collective-permute-done | bytes 73760 | tf_op jit(solution)/shard_map/ppermute | solution.py:557
  24.8 1.1 %blend.1 = (bf16[32,1024]{1,0:T(8,128)(2,1)S(1)}, bf16[32,1152]{1,0:T(8,128)(2,1)S(1)}, bf16[32,1152]{1,0:T(8,128)(2,1)S(1)}) custom-call(bf16[1024,4608]{1,0:T(8,128)(2,1)S(1)} %bitcast.6, f32[32,1152]{1,0:T(8,128)S(1)} %get-tuple-element.19.own_ref, f32[32,1152]{1,0:T(8,128)S(1)} %get-tuple-element.22.self_ref, ...), custom_call_target="tpu_custom_call" | custom-call | flops 751619264 | bytes 734003 | tf_op jit(solution)/shard_map/blend/pallas_call | solution.py:688
  25.9 3.2 %collective-permute-start.6 = (bf16[32,1152]{1,0:T(8,128)(2,1)S(1)}, bf16[32,1152]{1,0:T(8,128)(2,1)S(1)}, u32[]{:S(2)}, u32[]{:S(2)}) collective-permute-start(bf16[32,1152]{1,0:T(8,128)(2,1)S(1)} %get-tuple-element.28), channel_id=1, source_target_pairs={{0,2},{1,3},{2,0},{3,1},{4,6},{5,7},{6,4},{7,5},{8,10},{9,11},{10,... | collective-permute-start | bytes 221192 | tf_op jit(solution)/shard_map/ppermute | solution.py:557
  29.1 1.3 %collective-permute-start.7 = (bf16[32,1152]{1,0:T(8,128)(2,1)S(1)}, bf16[32,1152]{1,0:T(8,128)(2,1)S(1)}, u32[]{:S(2)}, u32[]{:S(2)}) collective-permute-start(bf16[32,1152]{1,0:T(8,128)(2,1)S(1)} %get-tuple-element.29), channel_id=1, source_target_pairs={{0,3},{1,2},{2,1},{3,0},{4,7},{5,6},{6,5},{7,4},{8,11},{9,10},{10,... | collective-permute-start | bytes 221192 | tf_op jit(solution)/shard_map/ppermute | solution.py:557
  30.4 0.9 %project.1 = (f32[32,1152]{1,0:T(8,128)S(1)}, bf16[32,1152]{1,0:T(8,128)(2,1)S(1)}) custom-call(bf16[1024,4608]{1,0:T(8,128)(2,1)S(1)} %bitcast.6, bf16[32,1024]{1,0:T(8,128)(2,1)S(1)} %get-tuple-element.25.att_ref), custom_call_target="tpu_custom_call" | custom-call | flops 1395864320 | bytes 1363148 | tf_op jit(solution)/shard_map/project/pallas_call | solution.py:699
  31.3 0.3 collective-permute-start.5
  31.7 2.2 %collective-permute-done.6.r2 = bf16[32,1152]{1,0:T(8,128)(2,1)S(1)} collective-permute-done((bf16[32,1152]{1,0:T(8,128)(2,1)S(1)}, bf16[32,1152]{1,0:T(8,128)(2,1)S(1)}, u32[]{:S(2)}, u32[]{:S(2)}) %collective-permute-start.6) | collective-permute-done | bytes 73760 | tf_op jit(solution)/shard_map/ppermute | solution.py:557
  33.8 1.9 %collective-permute-done.7.r3 = bf16[32,1152]{1,0:T(8,128)(2,1)S(1)} collective-permute-done((bf16[32,1152]{1,0:T(8,128)(2,1)S(1)}, bf16[32,1152]{1,0:T(8,128)(2,1)S(1)}, u32[]{:S(2)}, u32[]{:S(2)}) %collective-permute-start.7) | collective-permute-done | bytes 73760 | tf_op jit(solution)/shard_map/ppermute | solution.py:557
  35.8 0.5 %collective-permute-done.5.r1 = bf16[32,1152]{1,0:T(8,128)(2,1)S(1)} collective-permute-done((bf16[32,1152]{1,0:T(8,128)(2,1)S(1)}, bf16[32,1152]{1,0:T(8,128)(2,1)S(1)}, u32[]{:S(2)}, u32[]{:S(2)}) %collective-permute-start.5) | collective-permute-done | bytes 73760 | tf_op jit(solution)/shard_map/ppermute | solution.py:557
  36.3 2.8 %collective-permute-start.10 = (f32[32,128]{1,0:T(8,128)S(1)}, f32[32,128]{1,0:T(8,128)S(1)}, u32[]{:S(2)}, u32[]{:S(2)}) collective-permute-start(f32[32,128]{1,0:T(8,128)S(1)} %get-tuple-element.31.s), channel_id=1, source_target_pairs={{0,3},{1,2},{2,1},{3,0},{4,7},{5,6},{6,5},{7,4},{8,11},{9,10},{10,... | collective-permute-start | bytes 49160 | tf_op jit(solution)/shard_map/ppermute | solution.py:557
  39.1 1.7 %collective-permute-start.8 = (f32[32,128]{1,0:T(8,128)S(1)}, f32[32,128]{1,0:T(8,128)S(1)}, u32[]{:S(2)}, u32[]{:S(2)}) collective-permute-start(f32[32,128]{1,0:T(8,128)S(1)} %get-tuple-element.31.s), channel_id=1, source_target_pairs={{0,1},{1,0},{2,3},{3,2},{4,5},{5,4},{6,7},{7,6},{8,9},{9,8},{10,11... | collective-permute-start | bytes 49160 | tf_op jit(solution)/shard_map/ppermute | solution.py:557
  40.8 0.7 %copy.15 = bf16[32,2,512]{2,1,0:T(2,128)(2,1)} copy(bf16[32,2,512]{2,0,1:T(8,128)(2,1)S(1)} %pad_maximum_fusion) | data formatting | bytes 131072
  41.5 0.4 collective-permute-done.10.r3
  42.0 1.8 %collective-permute-done.9.r2 = f32[32,128]{1,0:T(8,128)S(1)} collective-permute-done((f32[32,128]{1,0:T(8,128)S(1)}, f32[32,128]{1,0:T(8,128)S(1)}, u32[]{:S(2)}, u32[]{:S(2)}) %collective-permute-start.9) | collective-permute-done | bytes 16416 | tf_op jit(solution)/shard_map/ppermute | solution.py:557
  43.8 0.7 %last.1 = bf16[32,1152]{1,0:T(8,128)(2,1)} custom-call(f32[32,1152]{1,0:T(8,128)S(1)} %get-tuple-element.30.t, f32[32,128]{1,0:T(8,128)S(1)} %get-tuple-element.31.s, f32[32,128]{1,0:T(8,128)S(1)} %collective-permute-done.8.r1, f32[32,128]{1,0:T(8,128)S(1)} %collective-permute-done.9.r2, f32[32,128]{1,0:T(8,128)S(1)} %collective-permute-done.10.r3, ...), custom_call_target="tpu_custom_call" | custom-call | flops 322122560 | bytes 314572 | tf_op jit(solution)/shard_map/last/pallas_call | solution.py:720
  (34 shorter events, 0.1 us)
Async XLA Ops:
  0.6 11.4 %copy-start.1 = (bf16[64,2,64,512]{3,2,1,0:T(8,128)(2,1)S(1)}, bf16[64,2,64,512]{3,2,1,0:T(8,128)(2,1)}, u32[]{:S(2)}) copy-start(bf16[64,2,64,512]{3,2,1,0:T(8,128)(2,1)} %rest_1_.1) | copy-start | bytes 25165828
  5.4 5.3 %copy-start.3 = (s32[128,32]{0,1:T(8,128)S(1)}, s32[128,32]{0,1:T(8,128)}, u32[]{:S(2)}) copy-start(s32[128,32]{0,1:T(8,128)} %param.23) | copy-start | bytes 49156
  5.4 5.3 %copy-start.4 = (s32[128]{0:T(128)S(1)}, s32[128]{0:T(128)}, u32[]{:S(2)}) copy-start(s32[128]{0:T(128)} %lens_hbm.1) | copy-start | bytes 1540
  5.4 5.3 %copy-start.5 = (s32[128]{0:T(128)S(1)}, s32[128]{0:T(128)}, u32[]{:S(2)}) copy-start(s32[128]{0:T(128)} %param.21) | copy-start | bytes 1540
  5.4 6.6 %copy-start = (bf16[64,2,128,512]{3,2,1,0:T(8,128)(2,1)S(1)}, bf16[64,2,128,512]{3,2,1,0:T(8,128)(2,1)}, u32[]{:S(2)}) copy-start(bf16[64,2,128,512]{3,2,1,0:T(8,128)(2,1)} %rest_0_.1) | copy-start | bytes 50331652
  5.5 5.3 %collective-permute-start.1 = (bf16[32,1024]{1,0:T(8,128)(2,1)S(1)}, bf16[32,1024]{1,0:T(8,128)(2,1)S(1)}, u32[]{:S(2)}, u32[]{:S(2)}) collective-permute-start(bf16[32,1024]{1,0:T(8,128)(2,1)S(1)} %gate.1.q0.q_ref), channel_id=1, source_target_pairs={{0,8},{4,12},{8,0},{12,4},{1,9},{5,13},{9,1},{13,5},{2,10},{6,14},... | collective-permute-start | bytes 196616 | tf_op jit(solution)/shard_map/ppermute | solution.py:557
  8.5 2.6 %collective-permute-start = (bf16[32,1024]{1,0:T(8,128)(2,1)S(1)}, bf16[32,1024]{1,0:T(8,128)(2,1)S(1)}, u32[]{:S(2)}, u32[]{:S(2)}) collective-permute-start(bf16[32,1024]{1,0:T(8,128)(2,1)S(1)} %gate.1.q0.q_ref), channel_id=1, source_target_pairs={{0,4},{4,0},{8,12},{12,8},{1,5},{5,1},{9,13},{13,9},{2,6},{6,2},{1... | collective-permute-start | bytes 196616 | tf_op jit(solution)/shard_map/ppermute | solution.py:557
  10.7 1.3 %collective-permute-start.2 = (bf16[32,1024]{1,0:T(8,128)(2,1)S(1)}, bf16[32,1024]{1,0:T(8,128)(2,1)S(1)}, u32[]{:S(2)}, u32[]{:S(2)}) collective-permute-start(bf16[32,1024]{1,0:T(8,128)(2,1)S(1)} %collective-permute-done.1.q2), channel_id=1, source_target_pairs={{0,4},{4,0},{8,12},{12,8},{1,5},{5,1},{9,13},{13,9},{2,6},{6,2},{1... | collective-permute-start | bytes 196616 | tf_op jit(solution)/shard_map/ppermute | solution.py:557
  10.8 11.4 %slice-start.3 = ((s8[4718592]{0:T(1024)(128)(4,1)}), s8[4194304]{0:T(1024)(128)(4,1)S(1)}, s32[]{:S(2)}) async-start(s8[4718592]{0:T(1024)(128)(4,1)} %bitcast.7), calls=%async_computation.3 | async-start | bytes 8388608
  10.8 11.4 %slice-start.5 = ((s8[4718592]{0:T(1024)(128)(4,1)}), s8[4194304]{0:T(1024)(128)(4,1)S(1)}, s32[]{:S(2)}) async-start(s8[4718592]{0:T(1024)(128)(4,1)} %bitcast.9), calls=%async_computation.5 | async-start | bytes 8388608
  10.8 14.0 %slice-start = ((s8[9437184]{0:T(1024)(128)(4,1)}), s8[4194304]{0:T(1024)(128)(4,1)S(1)}, s32[]{:S(2)}) async-start(s8[9437184]{0:T(1024)(128)(4,1)} %bitcast.5), calls=%async_computation | async-start | bytes 8388608
  11.1 11.1 %slice-start.4 = ((s8[4718592]{0:T(1024)(128)(4,1)}), s8[524288]{0:T(1024)(128)(4,1)S(1)}, s32[]{:S(2)}) async-start(s8[4718592]{0:T(1024)(128)(4,1)} %bitcast.7), calls=%async_computation.4 | async-start | bytes 1048576
  11.1 11.1 %slice-start.6 = ((s8[4718592]{0:T(1024)(128)(4,1)}), s8[524288]{0:T(1024)(128)(4,1)S(1)}, s32[]{:S(2)}) async-start(s8[4718592]{0:T(1024)(128)(4,1)} %bitcast.9), calls=%async_computation.6 | async-start | bytes 1048576
  11.1 13.7 %slice-start.1 = ((s8[9437184]{0:T(1024)(128)(4,1)}), s8[4194304]{0:T(1024)(128)(4,1)S(1)}, s32[]{:S(2)}) async-start(s8[9437184]{0:T(1024)(128)(4,1)} %bitcast.5), calls=%async_computation.1 | async-start | bytes 8388608
  11.1 13.6 %slice-start.2 = ((s8[9437184]{0:T(1024)(128)(4,1)}), s8[1048576]{0:T(1024)(128)(4,1)S(1)}, s32[]{:S(2)}) async-start(s8[9437184]{0:T(1024)(128)(4,1)} %bitcast.5), calls=%async_computation.2 | async-start | bytes 2097152
  17.6 2.2 %collective-permute-start.3 = (bf16[64,1152]{1,0:T(8,128)(2,1)S(1)}, bf16[64,1152]{1,0:T(8,128)(2,1)S(1)}, u32[]{:S(2)}, u32[]{:S(2)}) collective-permute-start(bf16[64,1152]{1,0:T(8,128)(2,1)S(1)} %get-tuple-element.23), channel_id=1, source_target_pairs={{0,4},{4,0},{8,12},{12,8},{1,5},{5,1},{9,13},{13,9},{2,6},{6,2},{1... | collective-permute-start | bytes 442376 | tf_op jit(solution)/shard_map/ppermute | solution.py:557
  20.0 4.8 %collective-permute-start.4 = (bf16[32,1152]{1,0:T(8,128)(2,1)S(1)}, bf16[32,1152]{1,0:T(8,128)(2,1)S(1)}, u32[]{:S(2)}, u32[]{:S(2)}) collective-permute-start(bf16[32,1152]{1,0:T(8,128)(2,1)S(1)} %merge.1), channel_id=1, source_target_pairs={{0,8},{4,12},{8,0},{12,4},{1,9},{5,13},{9,1},{13,5},{2,10},{6,14},... | collective-permute-start | bytes 221192 | tf_op jit(solution)/shard_map/ppermute | solution.py:557
  24.8 16.0 %copy-start.6 = (f32[1152]{0:T(1024)S(1)}, f32[1152]{0:T(1024)}, u32[]{:S(2)}) copy-start(f32[1152]{0:T(1024)} %param.18) | copy-start | bytes 13828
  24.8 19.0 %copy-start.2 = (bf16[32,4608]{1,0:T(8,128)(2,1)S(1)}, bf16[32,4608]{1,0:T(8,128)(2,1)}, u32[]{:S(2)}) copy-start(bf16[32,4608]{1,0:T(8,128)(2,1)} %hd.1) | copy-start | bytes 884740
  25.9 8.0 %collective-permute-start.6 = (bf16[32,1152]{1,0:T(8,128)(2,1)S(1)}, bf16[32,1152]{1,0:T(8,128)(2,1)S(1)}, u32[]{:S(2)}, u32[]{:S(2)}) collective-permute-start(bf16[32,1152]{1,0:T(8,128)(2,1)S(1)} %get-tuple-element.28), channel_id=1, source_target_pairs={{0,2},{1,3},{2,0},{3,1},{4,6},{5,7},{6,4},{7,5},{8,10},{9,11},{10,... | collective-permute-start | bytes 221192 | tf_op jit(solution)/shard_map/ppermute | solution.py:557
  29.1 6.7 %collective-permute-start.7 = (bf16[32,1152]{1,0:T(8,128)(2,1)S(1)}, bf16[32,1152]{1,0:T(8,128)(2,1)S(1)}, u32[]{:S(2)}, u32[]{:S(2)}) collective-permute-start(bf16[32,1152]{1,0:T(8,128)(2,1)S(1)} %get-tuple-element.29), channel_id=1, source_target_pairs={{0,3},{1,2},{2,1},{3,0},{4,7},{5,6},{6,5},{7,4},{8,11},{9,10},{10,... | collective-permute-start | bytes 221192 | tf_op jit(solution)/shard_map/ppermute | solution.py:557
  31.3 4.9 %collective-permute-start.5 = (bf16[32,1152]{1,0:T(8,128)(2,1)S(1)}, bf16[32,1152]{1,0:T(8,128)(2,1)S(1)}, u32[]{:S(2)}, u32[]{:S(2)}) collective-permute-start(bf16[32,1152]{1,0:T(8,128)(2,1)S(1)} %get-tuple-element.27), channel_id=1, source_target_pairs={{0,1},{1,0},{2,3},{3,2},{4,5},{5,4},{6,7},{7,6},{8,9},{9,8},{10,11... | collective-permute-start | bytes 221192 | tf_op jit(solution)/shard_map/ppermute | solution.py:557
  36.3 5.6 %collective-permute-start.10 = (f32[32,128]{1,0:T(8,128)S(1)}, f32[32,128]{1,0:T(8,128)S(1)}, u32[]{:S(2)}, u32[]{:S(2)}) collective-permute-start(f32[32,128]{1,0:T(8,128)S(1)} %get-tuple-element.31.s), channel_id=1, source_target_pairs={{0,3},{1,2},{2,1},{3,0},{4,7},{5,6},{6,5},{7,4},{8,11},{9,10},{10,... | collective-permute-start | bytes 49160 | tf_op jit(solution)/shard_map/ppermute | solution.py:557
  39.1 4.6 %collective-permute-start.9 = (f32[32,128]{1,0:T(8,128)S(1)}, f32[32,128]{1,0:T(8,128)S(1)}, u32[]{:S(2)}, u32[]{:S(2)}) collective-permute-start(f32[32,128]{1,0:T(8,128)S(1)} %get-tuple-element.31.s), channel_id=1, source_target_pairs={{0,2},{1,3},{2,0},{3,1},{4,6},{5,7},{6,4},{7,5},{8,10},{9,11},{10,... | collective-permute-start | bytes 49160 | tf_op jit(solution)/shard_map/ppermute | solution.py:557
  39.1 4.6 %collective-permute-start.8 = (f32[32,128]{1,0:T(8,128)S(1)}, f32[32,128]{1,0:T(8,128)S(1)}, u32[]{:S(2)}, u32[]{:S(2)}) collective-permute-start(f32[32,128]{1,0:T(8,128)S(1)} %get-tuple-element.31.s), channel_id=1, source_target_pairs={{0,1},{1,0},{2,3},{3,2},{4,5},{5,4},{6,7},{7,6},{8,9},{9,8},{10,11... | collective-permute-start | bytes 49160 | tf_op jit(solution)/shard_map/ppermute | solution.py:557
